TPU v7x, 32 devices: a whole 2x2x4 slice. The times are simulated.
32 devices in a mesh: sweep: 2 (over y), seq: 8 (over z, x), head: 2 (over core).
Axes of the slice: x: 2, y: 2, z: 4, core: 2. Of those that a mesh axis runs over, the one named last changes fastest.
Arguments:
- queries: bfloat16 [2048, 1024], P(('sweep', 'seq'), 'head'), parts along dimension 0, may hold values from -6 to 6
- key_matrix: bfloat16 [2048, 256], P(('sweep', 'seq'), 'head'), parts along dimension 0, may hold values from -6 to 6
- value_matrix: bfloat16 [2048, 256], P(('sweep', 'seq'), 'head'), parts along dimension 0, may hold values from -6 to 6
- segment_ids: int32 [2048], P(('sweep', 'seq')), parts along dimension 0, may hold values from 0 to 16, as said below
Outputs:
- attended: bfloat16 [2048, 1024], P(('sweep', 'seq'), 'head'), parts along dimension 0
There are 2 independent parts, one for each index of `sweep`. A program takes and returns all parts, laid end to end along the dimension named above; each array names one. Nothing has to cross between parts.
Inputs may be any that keep to these rules, and one draw needn't show every extreme that they name: `segment_ids`: never falling. Segment 0 is a prompt at the start of 128 to 256 tokens; each id of 1 to 16 is one response of one or more tokens.
All inputs are finite; a program needn't handle non-finite values.
Results may differ from a plain program's by a relative error of at most 0.005.
Values may be sent and summed in bfloat16 or wider, within the bound.
No kernel may reach another device: no remote copies, remote signals or barrier semaphores. Data moves between devices by JAX's collectives and lax.ppermute only.
A program may use at most 64 MiB of HBM per device.

v0:
```python
import math

import jax
import jax.numpy as jnp
from jax import lax
from jax.sharding import PartitionSpec as P

HEAD_WIDTH = 64


NEG_FILL = -1e30


def attend_block(state, query_heads, query_pos, query_seg, key_blk, value_blk, seg_blk, key_start):
    run_max, weight_total, totals = state
    groups = query_heads.shape[1]
    head_size = query_heads.shape[3]
    count = key_blk.shape[0]
    key_pos = key_start + jnp.arange(count, dtype=jnp.int32)
    visible = (key_pos[None, :] <= query_pos[:, None]) & (
        (seg_blk[None, :] == query_seg[:, None]) | (seg_blk[None, :] == 0)
    )

    def update(unused):
        logit_scores = jnp.einsum(
            "opez,hpz->peoh",
            query_heads,
            key_blk.reshape(count, groups, head_size),
            preferred_element_type=jnp.float32,
        ) * (1.0 / math.sqrt(head_size))
        logit_scores = jnp.where(visible, logit_scores, NEG_FILL)
        new_max = jnp.maximum(run_max, jnp.max(logit_scores, axis=-1))
        weights = jnp.where(visible, jnp.exp(logit_scores - new_max[..., None]), 0.0)
        rescale = jnp.exp(run_max - new_max)
        new_sum = weight_total * rescale + jnp.sum(weights, axis=-1)
        mixed_output = jnp.einsum(
            "omhy,yoc->omhc",
            weights.astype(jnp.bfloat16),
            value_blk.reshape(count, groups, head_size),
            preferred_element_type=jnp.float32,
        )
        return (new_max, new_sum, totals * rescale[..., None] + mixed_output)

    def keep(unused):
        return state

    return lax.cond(jnp.any(visible), update, keep, 0)


def build_fold(query_sets):

    def apply_all(states, key_piece, value_piece, seg_piece, start):
        return tuple(
            (
                attend_block(
                    states[number],
                    entry[0],
                    entry[1],
                    entry[2],
                    key_piece,
                    value_piece,
                    seg_piece,
                    start,
                )
                for number, entry in enumerate(query_sets)
            )
        )

    def fold(states, piece, start):
        key_piece, value_piece, seg_piece = piece
        rows = key_piece.shape[0]
        width = 512

        def loop_step(index, carried):
            offset = index * width
            return apply_all(
                carried,
                lax.dynamic_slice_in_dim(key_piece, offset, width, 0),
                lax.dynamic_slice_in_dim(value_piece, offset, width, 0),
                lax.dynamic_slice_in_dim(seg_piece, offset, width, 0),
                offset,
            )

        return lax.fori_loop(0, rows // width, loop_step, states)

    return fold


def start_state(query_heads):
    tok_rows, groups, repeat_factor, head_size = query_heads.shape
    return (
        jnp.full((groups, repeat_factor, tok_rows), NEG_FILL, jnp.float32),
        jnp.zeros((groups, repeat_factor, tok_rows), jnp.float32),
        jnp.zeros((groups, repeat_factor, tok_rows, head_size), jnp.float32),
    )


def finish(state):
    run_max, weight_total, totals = state
    result = totals / weight_total[..., None]
    groups, repeat_factor, tok_rows, head_size = result.shape
    return (
        jnp.transpose(result, (2, 0, 1, 3))
        .reshape(tok_rows, groups * repeat_factor * head_size)
        .astype(jnp.bfloat16)
    )


def per_device(queries, key_matrix, value_matrix, segment_ids):
    head_size = HEAD_WIDTH
    block_rows = segment_ids.shape[0]
    groups = key_matrix.shape[1] // head_size
    repeat_factor = queries.shape[1] // head_size // groups
    position = lax.axis_index("seq")
    query_pos = position * block_rows + jnp.arange(block_rows, dtype=jnp.int32)
    query_sets = (
        (queries.reshape(block_rows, groups, repeat_factor, head_size), query_pos, segment_ids),
    )
    fold = build_fold(query_sets)
    states = tuple((start_state(entry[0]) for entry in query_sets))
    states = fold(
        states,
        (
            lax.all_gather(key_matrix, "seq", axis=0, tiled=True),
            lax.all_gather(value_matrix, "seq", axis=0, tiled=True),
            lax.all_gather(segment_ids, "seq", axis=0, tiled=True),
        ),
        jnp.int32(0),
    )
    return finish(states[0])


def solution(mesh):
    in_specs = (
        P(("sweep", "seq"), "head"),
        P(("sweep", "seq"), "head"),
        P(("sweep", "seq"), "head"),
        P(("sweep", "seq")),
    )
    out_specs = P(("sweep", "seq"), "head")
    return jax.shard_map(
        per_device, mesh=mesh, in_specs=in_specs, out_specs=out_specs, check_vma=False
    )
```

profile of v0, /device:TPU:0, one launch (start us, length us, event | category | flops | bytes accessed | tf_op | source)
XLA Modules:
  0.0 85.6 jit_solution(3842779649709735597)
XLA Ops:
  0.0 22.4 %all-gather = s32[8,1,128]{2,1,0:T(1,128)S(1)} all-gather(s32[1,1,128]{2,1,0:T(1,128)} %bitcast.47), channel_id=1, replica_groups=mesh['sweep'=2,'seq'=8,'head'=2] {'seq'}, dimensions={0}, use_global_device_ids=true | all-gather | bytes 4608 | tf_op jit(solution)/shard_map/all_gather | solution.py:126
  22.4 0.9 %copy.16 = bf16[128,128]{0,1:T(8,128)(2,1)S(1)} copy(bf16[128,128]{1,0:T(8,128)(2,1)} %param.9) | data formatting | bytes 65536 | tf_op args[1]
  23.3 0.9 %copy.18 = bf16[128,128]{0,1:T(8,128)(2,1)S(1)} copy(bf16[128,128]{1,0:T(8,128)(2,1)} %param.10) | data formatting | bytes 65536 | tf_op args[2]
  24.2 1.0 %copy.17 = bf16[128,512]{0,1:T(8,128)(2,1)S(1)} copy(bf16[128,512]{1,0:T(8,128)(2,1)} %param.8) | data formatting | bytes 262144 | tf_op args[0]
  25.2 26.7 %all_gather.11 = bf16[1024,128]{0,1:T(8,128)(2,1)S(1)} all-gather(bf16[128,128]{0,1:T(8,128)(2,1)S(1)} %copy.18), channel_id=1, replica_groups=mesh['sweep'=2,'seq'=8,'head'=2] {'seq'}, dimensions={0}, use_global_device_ids=true | all-gather | bytes 294912 | tf_op jit(solution)/shard_map/all_gather | solution.py:125
  51.9 26.4 %all_gather.10 = bf16[1024,128]{0,1:T(8,128)(2,1)S(1)} all-gather(bf16[128,128]{0,1:T(8,128)(2,1)S(1)} %copy.16), channel_id=1, replica_groups=mesh['sweep'=2,'seq'=8,'head'=2] {'seq'}, dimensions={0}, use_global_device_ids=true | all-gather | bytes 294912 | tf_op jit(solution)/shard_map/all_gather | solution.py:124
  78.4 6.5 %while.18 = (s32[]{:T(128)}, f32[2,4,128]{2,1,0:T(4,128)S(1)}, f32[2,4,128]{2,1,0:T(4,128)S(1)}, f32[2,4,128,64]{2,3,1,0:T(8,128)S(1)}, s32[1024]{0:T(1024)S(1)}...) while((s32[]{:T(128)}, f32[2,4,128]{2,1,0:T(4,128)S(1)}, ...), condition=%wide.region_6.7_spmd.clone, body=%wide.region_0.6_spmd.clone.sunk | while | flops 141495424 | bytes 8074049 | solution.py:84
  78.4 0.1 broadcast_compare_fusion.2
  78.5 1.6 %fusion.18 = (pred[]{:T(512)}, pred[128,512]{0,1:T(8,128)(4,1)S(1)}) fusion(pred[512]{0:T(512)(128)(4,1)S(1)} %get-tuple-element.383, s32[128]{0:T(128)} %get-tuple-element.429, s32[512]{0:T(512)S(1)} %get-tuple-element.384, s32[128]{0:T(128)S(1)} %iota_add_fusion.4, s32[512]{0:T(512)S(1)} %iota_add_fusion.5), kind=kLoop, calls=%fused_computation.23.clone.1 | loop fusion | flops 327679 | bytes 71169 | tf_op jit(solution)/shard_map/while/body/eval_jaxpr/reduce_or | solution.py:47
  80.7 1.8 %conditional.3 = ((f32[2,4,128]{2,1,0:T(4,128)S(1)}, f32[2,4,128]{2,1,0:T(4,128)S(1)}, f32[2,4,128,64]{2,3,1,0:T(8,128)S(1)})) conditional(s32[]{:T(128)} %convert_element_type.29, (f32[2,4,128]{2,1,0:T(4,128)S(1)}, f32[2,4,128]{2,1,0:T(4,128)S(1)}, f32[2,4,128,64]{2,3,1,0:T(8,128)S(1)}) %tuple.56, (pred[128,512]{0,1:T(8,128)(4,1)S(1)}, ...), branch_computations={%region_2.0_spmd, %region_3.5_spmd} | conditional | flops 141166592 | bytes 7995428 | solution.py:47
  80.8 0.5 fusion.2
  81.3 0.5 fusion.4
  81.8 0.6 convolution_add_fusion
  82.5 0.1 broadcast_compare_fusion.2
  82.6 1.6 %fusion.18 = (pred[]{:T(512)}, pred[128,512]{0,1:T(8,128)(4,1)S(1)}) fusion(pred[512]{0:T(512)(128)(4,1)S(1)} %get-tuple-element.383, s32[128]{0:T(128)} %get-tuple-element.429, s32[512]{0:T(512)S(1)} %get-tuple-element.384, s32[128]{0:T(128)S(1)} %iota_add_fusion.4, s32[512]{0:T(512)S(1)} %iota_add_fusion.5), kind=kLoop, calls=%fused_computation.23.clone.1 | loop fusion | flops 327679 | bytes 71169 | tf_op jit(solution)/shard_map/while/body/eval_jaxpr/reduce_or | solution.py:47
  84.9 0.8 copy.19
  (13 shorter events, 0.1 us)
where the time goes:
time: 86 us; the launch traced here: 85.6 us
  blocking collectives  75.6 us (88%)
  other arithmetic  3.92 us (5%)
  local copies, waits for them, and re-layouts  3.59 us (4%)
  loops' own time  1.39 us (2%)
  matrix products  1.15 us (1%)
    all_gather x1, blocking collectives, per_device(): lax.all_gather(value_matrix, 'seq', axis=0, tiled=True)  26.7 us
    all_gather x1, blocking collectives, per_device(): lax.all_gather(key_matrix, 'seq', axis=0, tiled=True)  26.4 us
    all_gather x1, blocking collectives, per_device(): lax.all_gather(segment_ids, 'seq', axis=0, tiled=True)  22.4 us
    reduce_or x2, other arithmetic, attend_block(): return lax.cond(jnp.any(visible), update, keep, 0)  3.19 us
    unnamed x3, local copies, waits for them, and re-layouts  2.76 us

commit v1 on v0

--- a/solution.py
+++ b/solution.py
@@ -1,14 +1,295 @@
+import functools
 import math
 
 import jax
 import jax.numpy as jnp
 from jax import lax
+from jax.experimental import pallas as pl
+from jax.experimental.pallas import tpu as pltpu
 from jax.sharding import PartitionSpec as P
 
+
 HEAD_WIDTH = 64
-
-
 NEG_FILL = -1e30
+SEG_ROWS = 8
+SMALL_VMEM = 1 << 20
+VMEM_LIMIT = 16 << 20
+VMEM = pl.BlockSpec(memory_space=pltpu.VMEM)
+HBM = pl.BlockSpec(memory_space=pltpu.HBM)
+
+
+def in_hbm(array):
+    return pltpu.with_memory_space_constraint(array, pltpu.HBM)
+
+
+def pack_kernel(k_ref, v_ref, seg_ref, out_ref, seg_buf, sems):
+    tokens, lanes = k_ref.shape
+    copies = [
+        pltpu.make_async_copy(seg_ref, seg_buf, sems.at[0]),
+        pltpu.make_async_copy(k_ref, out_ref.at[:tokens, :lanes], sems.at[1]),
+        pltpu.make_async_copy(v_ref, out_ref.at[:tokens, lanes:], sems.at[2]),
+    ]
+    for copy in copies:
+        copy.start()
+    copies[0].wait()
+    row = jnp.broadcast_to(seg_buf[...].astype(jnp.float32), (SEG_ROWS, tokens)).astype(jnp.bfloat16)
+    out_ref[tokens:, :lanes] = row
+    out_ref[tokens:, lanes:] = row
+    copies[1].wait()
+    copies[2].wait()
+
+
+def pack(key_matrix, value_matrix, seg_row):
+    tokens, lanes = key_matrix.shape
+    return pl.pallas_call(
+        pack_kernel,
+        out_shape=pltpu.VMEM((tokens + SEG_ROWS, 2 * lanes), key_matrix.dtype),
+        in_specs=[HBM] * 3,
+        out_specs=VMEM,
+        scratch_shapes=[pltpu.VMEM((1, tokens), jnp.int32), pltpu.SemaphoreType.DMA((3,))],
+        compiler_params=pltpu.CompilerParams(vmem_limit_bytes=SMALL_VMEM),
+        name="pack",
+    )(in_hbm(key_matrix), in_hbm(value_matrix), in_hbm(seg_row))
+
+
+def joined(pieces, first, width, tokens):
+    parts = [piece[:tokens, first : first + width] for piece in pieces]
+    return parts[0] if len(parts) == 1 else jnp.concatenate(parts, axis=0)
+
+
+def seg_grid(piece, tokens):
+    line = piece[tokens : tokens + SEG_ROWS, :tokens].astype(jnp.float32)[0:1]
+    return jnp.broadcast_to(line, (tokens, tokens))
+
+
+def bias_of(me, step, piece, query_seg):
+    tokens = query_seg.shape[0]
+    key_seg = seg_grid(piece, tokens)
+    if step == 0:
+        row = lax.broadcasted_iota(jnp.int32, (tokens, tokens), 0)
+        col = lax.broadcasted_iota(jnp.int32, (tokens, tokens), 1)
+        seen = ((key_seg == query_seg) | (key_seg == 0.0)) & (col <= row)
+    else:
+        if step == 1:
+            key_seg = jnp.where((me ^ step) < me, key_seg, -1.0)
+        seen = (key_seg == query_seg) | (key_seg == 0.0)
+    return jnp.where(seen, 0.0, NEG_FILL)
+
+
+def folded(values, tokens, op):
+    parts = [values[:, at : at + tokens] for at in range(0, values.shape[1], tokens)]
+    return functools.reduce(op, parts)
+
+
+def attend(me, blocks, query_seg, q_all, scores, heads, factor, lanes, before, after):
+    tokens = query_seg.shape[0]
+    query_rows = q_all[...]
+    biases, value_blocks = [], []
+    for number, block in enumerate(blocks):
+        members = [piece for _, piece in block]
+        scores[number, :, : len(block) * tokens] = lax.dot_general(
+            query_rows, joined(members, 0, lanes, tokens), (((1,), (1,)), ((), ())),
+            preferred_element_type=jnp.float32,
+        )
+        parts = [bias_of(me, step, piece, query_seg) for step, piece in block]
+        biases.append(parts[0] if len(parts) == 1 else jnp.concatenate(parts, axis=1))
+        value_blocks.append(joined(members, lanes, lanes, tokens))
+    for head in range(heads):
+        rows = slice(head * tokens, (head + 1) * tokens)
+        state = before(rows)
+        masked = []
+        high = None if state is None else state[0]
+        for number, block in enumerate(blocks):
+            part = scores[number, rows, : len(block) * tokens] + biases[number]
+            masked.append(part)
+            part = folded(part, tokens, jnp.maximum)
+            high = part if high is None else jnp.maximum(high, part)
+        top = jnp.max(high, axis=1, keepdims=True)
+        total = mixed = None
+        if state is not None:
+            rescale = jnp.exp2((state[0] - top) * factor)
+            total, mixed = state[1] * rescale, state[2] * rescale
+        for part, value_block in zip(masked, value_blocks):
+            weights = jnp.exp2((part - top) * factor)
+            share = folded(weights, tokens, jnp.add)
+            total = share if total is None else total + share
+            product = jnp.dot(
+                weights.astype(jnp.bfloat16), value_block, preferred_element_type=jnp.float32
+            )
+            mixed = product if mixed is None else mixed + product
+        after(head, rows, top, total, mixed)
+
+
+def assemble(results, repeat, width, lanes, out_buf):
+    tokens = out_buf.shape[0]
+    lane = lax.broadcasted_iota(jnp.int32, (tokens, lanes), 1)
+    per_tile = lanes // width
+    for tile in range(len(results) // per_tile):
+        whole = None
+        for slot in range(per_tile):
+            head = tile * per_tile + slot
+            shift = (slot * width - head // repeat * width) % lanes
+            value = results[head]
+            if shift:
+                value = pltpu.roll(value, shift, 1)
+            whole = value if whole is None else jnp.where(lane >= slot * width, value, whole)
+        out_buf[:, tile * lanes : (tile + 1) * lanes] = whole.astype(jnp.bfloat16)
+
+
+def normal(total, mixed):
+    return mixed * (1.0 / jnp.sum(total, axis=1, keepdims=True))
+
+
+def paired(items):
+    return [items[at : at + 2] for at in range(0, len(items), 2)]
+
+
+def seen_steps(pair, count):
+    return [step for step in range(2, count, 2) if pair ^ (step >> 1) < pair]
+
+
+def near_kernel(groups, repeat, count, *refs):
+    steps = [0, 1] + list(range(2, count, 2))
+    q_hbm, pieces = refs[0], dict(zip(steps, refs[1 : 1 + len(steps)]))
+    q_all, seg_ref, top_ref, sum_ref, mix_ref, out_hbm, q_buf, scores, sem = refs[1 + len(steps) :]
+    tokens, _ = q_buf.shape
+    lanes = q_all.shape[1]
+    width = lanes // groups
+    heads = groups * repeat
+    factor = math.log2(math.e) / math.sqrt(width)
+    me = lax.axis_index("seq")
+
+    copy = pltpu.make_async_copy(q_hbm, q_buf, sem)
+    copy.start()
+    query_seg = jnp.transpose(seg_grid(pieces[0], tokens))
+    seg_ref[...] = query_seg
+    lane = lax.broadcasted_iota(jnp.int32, (tokens, lanes), 1)
+    copy.wait()
+    for head in range(heads):
+        group = head // repeat
+        first = head * width // lanes * lanes
+        tile = q_buf[:, first : first + lanes].astype(jnp.float32)
+        shift = (group * width - (head * width - first)) % lanes
+        if shift:
+            tile = pltpu.roll(tile, shift, 1)
+        keep = (lane >= group * width) & (lane < (group + 1) * width)
+        q_all[head * tokens : (head + 1) * tokens, :] = jnp.where(keep, tile, 0.0).astype(jnp.bfloat16)
+
+    for pair in range(count // 2):
+
+        @pl.when(me // 2 == pair)
+        def _(pair=pair):
+            early = seen_steps(pair, count)
+            chosen = [0, 1] + early[len(early) % 2 :] + early[: len(early) % 2]
+            blocks = paired([(step, pieces[step]) for step in chosen])
+            results = []
+
+            def after(head, rows, top, total, mixed):
+                if early:
+                    top_ref[rows, :] = jnp.broadcast_to(top, (tokens, lanes))
+                    sum_ref[rows, :] = total
+                    mix_ref[rows, :] = mixed
+                else:
+                    results.append(normal(total, mixed))
+
+            attend(me, blocks, query_seg, q_all, scores, heads, factor, lanes, lambda rows: None, after)
+            if not early:
+                assemble(results, repeat, width, lanes, q_buf)
+                out_copy = pltpu.make_async_copy(q_buf, out_hbm, sem)
+                out_copy.start()
+                out_copy.wait()
+
+
+def far_kernel(groups, repeat, count, *refs):
+    steps = list(range(3, count, 2))
+    q_all, seg_ref, top_ref, sum_ref, mix_ref, out_in = refs[:6]
+    pieces = dict(zip(steps, refs[6 : 6 + len(steps)]))
+    out_hbm, out_buf, scores, sem = refs[6 + len(steps) :]
+    del out_in
+    lanes = q_all.shape[1]
+    width = lanes // groups
+    heads = groups * repeat
+    factor = math.log2(math.e) / math.sqrt(width)
+    me = lax.axis_index("seq")
+
+    for pair in range(1, count // 2):
+
+        @pl.when(me // 2 == pair)
+        def _(pair=pair):
+            blocks = paired([(step + 1, pieces[step + 1]) for step in seen_steps(pair, count)])
+            results = []
+
+            def before(rows):
+                return top_ref[rows, :], sum_ref[rows, :], mix_ref[rows, :]
+
+            def after(head, rows, top, total, mixed):
+                results.append(normal(total, mixed))
+
+            attend(me, blocks, seg_ref[...], q_all, scores, heads, factor, lanes, before, after)
+            assemble(results, repeat, width, lanes, out_buf)
+            out_copy = pltpu.make_async_copy(out_buf, out_hbm, sem)
+            out_copy.start()
+            out_copy.wait()
+
+
+def plan_of(count):
+    powers = [1 << bit for bit in range(1, count.bit_length() - 1)]
+    plan = [(step, 0, step) for step in reversed(powers)] + [(1, 0, 1)]
+    for step in range(2, count, 2):
+        if step not in powers:
+            low = step & -step
+            plan.append((step, step ^ low, low))
+    plan += [(step + 1, step, 1) for step in range(2, count, 2)]
+    return plan
+
+
+def per_device(count, queries, key_matrix, value_matrix, segment_ids):
+    tokens, lanes = key_matrix.shape
+    groups = lanes // HEAD_WIDTH
+    repeat = queries.shape[1] // HEAD_WIDTH // groups
+    heads = groups * repeat
+    plan = plan_of(count)
+    held = {0: pack(key_matrix, value_matrix, segment_ids.reshape(1, tokens))}
+    for step, source, mask in plan:
+        held[step] = lax.ppermute(held[source], "seq", [(i, i ^ mask) for i in range(count)])
+    near = [0, 1] + list(range(2, count, 2))
+    far = list(range(3, count, 2))
+    row_shape = (heads * tokens, lanes)
+    score_shape = (heads * tokens, 2 * tokens)
+    *state, out = pl.pallas_call(
+        functools.partial(near_kernel, groups, repeat, count),
+        out_shape=[
+            pltpu.VMEM(row_shape, jnp.bfloat16),
+            pltpu.VMEM((tokens, tokens), jnp.float32),
+            pltpu.VMEM(row_shape, jnp.float32),
+            pltpu.VMEM(row_shape, jnp.float32),
+            pltpu.VMEM(row_shape, jnp.float32),
+            pltpu.HBM(queries.shape, queries.dtype),
+        ],
+        in_specs=[HBM] + [VMEM] * len(near),
+        out_specs=[VMEM] * 5 + [HBM],
+        scratch_shapes=[
+            pltpu.VMEM(queries.shape, queries.dtype),
+            pltpu.VMEM(((len(near) + 1) // 2,) + score_shape, jnp.float32),
+            pltpu.SemaphoreType.DMA,
+        ],
+        compiler_params=pltpu.CompilerParams(vmem_limit_bytes=VMEM_LIMIT),
+        name="near",
+    )(in_hbm(queries), *[held[step] for step in near])
+    return pl.pallas_call(
+        functools.partial(far_kernel, groups, repeat, count),
+        out_shape=pltpu.HBM(queries.shape, queries.dtype),
+        in_specs=[VMEM] * 5 + [HBM] + [VMEM] * len(far),
+        out_specs=HBM,
+        scratch_shapes=[
+            pltpu.VMEM(queries.shape, queries.dtype),
+            pltpu.VMEM(((len(far) + 1) // 2,) + score_shape, jnp.float32),
+            pltpu.SemaphoreType.DMA,
+        ],
+        input_output_aliases={5: 0},
+        compiler_params=pltpu.CompilerParams(vmem_limit_bytes=VMEM_LIMIT),
+        name="far",
+    )(*state, out, *[held[step] for step in far])
 
 
 def attend_block(state, query_heads, query_pos, query_seg, key_blk, value_blk, seg_blk, key_start):
@@ -96,7 +377,7 @@
 
 
 def finish(state):
-    run_max, weight_total, totals = state
+    _, weight_total, totals = state
     result = totals / weight_total[..., None]
     groups, repeat_factor, tok_rows, head_size = result.shape
     return (
@@ -106,7 +387,7 @@
     )
 
 
-def per_device(queries, key_matrix, value_matrix, segment_ids):
+def per_device_general(queries, key_matrix, value_matrix, segment_ids):
     head_size = HEAD_WIDTH
     block_rows = segment_ids.shape[0]
     groups = key_matrix.shape[1] // head_size
@@ -130,14 +411,30 @@
     return finish(states[0])
 
 
+def paired_axis(count):
+    return 8 <= count <= 16 and count & (count - 1) == 0
+
+
+def suits(count, queries, key_matrix):
+    tokens, lanes = key_matrix.shape
+    return (
+        paired_axis(count)
+        and tokens == lanes == 2 * HEAD_WIDTH
+        and queries.shape[1] % lanes == 0
+    )
+
+
+def per_device_any(count, queries, key_matrix, value_matrix, segment_ids):
+    body = functools.partial(per_device, count)
+    if not suits(count, queries, key_matrix):
+        body = per_device_general
+    return body(queries, key_matrix, value_matrix, segment_ids)
+
+
 def solution(mesh):
-    in_specs = (
-        P(("sweep", "seq"), "head"),
-        P(("sweep", "seq"), "head"),
-        P(("sweep", "seq"), "head"),
-        P(("sweep", "seq")),
-    )
-    out_specs = P(("sweep", "seq"), "head")
+    count = mesh.shape["seq"]
+    in_specs = (P(("sweep", "seq"), "head"),) * 3 + (P(("sweep", "seq")),)
     return jax.shard_map(
-        per_device, mesh=mesh, in_specs=in_specs, out_specs=out_specs, check_vma=False
-    )
+        functools.partial(per_device_any, count),
+        mesh=mesh, in_specs=in_specs, out_specs=P(("sweep", "seq"), "head"), check_vma=False,
+    )

time: 86 us -> 18.9 us (0.22)
  the two profiles are of different devices: /device:TPU:0 before, /device:TPU:16 now
where the time goes in v1:
time: 18.9 us; the launch traced here: 18.7 us
  starting transfers between devices  8.01 us (42%)
  waiting for transfers between devices  6.16 us (33%)
  Pallas kernels  4.53 us (24%)
    ppermute x7, starting transfers between devices, per_device(): lax.ppermute(held[source], 'seq', [(i, i ^ mask) for i in range(count)])  8.01 us
    ppermute x7, waiting for transfers between devices, per_device(): lax.ppermute(held[source], 'seq', [(i, i ^ mask) for i in range(count)])  6.16 us
    pallas_call x1, Pallas kernels, per_device(): pl.pallas_call(functools.partial(near_kernel, groups, repeat, count), out...  2.12 us
    pallas_call x1, Pallas kernels, per_device(): pl.pallas_call(functools.partial(far_kernel, groups, repeat, count), out_...  1.6 us
    pallas_call x1, Pallas kernels, pack(): pl.pallas_call(pack_kernel, out_shape=pltpu.VMEM((tokens + SEG_ROWS, 2 *...  0.81 us
  transfers between devices with their start and end apart: 7, of which 4 were waited for; matrix products, arithmetic and copies ran while one was open for 0% of the time, Pallas kernels for 11%

profile of v1, /device:TPU:16, one launch (start us, length us, event | category | flops | bytes accessed | tf_op | source)
XLA Modules:
  0.0 18.7 jit_solution(8924703180132520119)
XLA Ops:
  0.0 0.8 %pack.1.refs_1_ = bf16[136,256]{1,0:T(8,128)(2,1)S(1)} custom-call(bf16[128,128]{1,0:T(8,128)(2,1)} %k_ref.1, bf16[128,128]{1,0:T(8,128)(2,1)} %v_ref.1, s32[1,128]{1,0:T(1,128)} %bitcast.1), custom_call_target="tpu_custom_call" | custom-call | tf_op jit(solution)/shard_map/pack/pallas_call | solution.py:44
  0.8 0.1 collective-permute-start.2
  0.9 1.9 %collective-permute-start.1 = (bf16[136,256]{1,0:T(8,128)(2,1)S(1)}, bf16[136,256]{1,0:T(8,128)(2,1)S(1)}, u32[]{:S(2)}, u32[]{:S(2)}) collective-permute-start(bf16[136,256]{1,0:T(8,128)(2,1)S(1)} %pack.1.refs_1_), channel_id=1, source_target_pairs={{0,4},{2,6},{4,0},{6,2},{8,12},{10,14},{12,8},{14,10},{1,5},{3,7},... | collective-permute-start | bytes 208904 | tf_op jit(solution)/shard_map/ppermute | solution.py:254
  2.8 3.9 %collective-permute-done.2.refs_4_ = bf16[136,256]{1,0:T(8,128)(2,1)S(1)} collective-permute-done((bf16[136,256]{1,0:T(8,128)(2,1)S(1)}, bf16[136,256]{1,0:T(8,128)(2,1)S(1)}, u32[]{:S(2)}, u32[]{:S(2)}) %collective-permute-start.2) | collective-permute-done | bytes 69664 | tf_op jit(solution)/shard_map/ppermute | solution.py:254
  6.7 2.0 %collective-permute-start.3 = (bf16[136,256]{1,0:T(8,128)(2,1)S(1)}, bf16[136,256]{1,0:T(8,128)(2,1)S(1)}, u32[]{:S(2)}, u32[]{:S(2)}) collective-permute-start(bf16[136,256]{1,0:T(8,128)(2,1)S(1)} %collective-permute-done.2.refs_4_), channel_id=1, source_target_pairs={{0,4},{2,6},{4,0},{6,2},{8,12},{10,14},{12,8},{14,10},{1,5},{3,7},... | collective-permute-start | bytes 208904 | tf_op jit(solution)/shard_map/ppermute | solution.py:254
  8.7 1.5 %collective-permute-start = (bf16[136,256]{1,0:T(8,128)(2,1)S(1)}, bf16[136,256]{1,0:T(8,128)(2,1)S(1)}, u32[]{:S(2)}, u32[]{:S(2)}) collective-permute-start(bf16[136,256]{1,0:T(8,128)(2,1)S(1)} %pack.1.refs_1_), channel_id=1, source_target_pairs={{0,2},{2,0},{4,6},{6,4},{8,10},{10,8},{12,14},{14,12},{1,3},{3,1},... | collective-permute-start | bytes 208904 | tf_op jit(solution)/shard_map/ppermute | solution.py:254
  10.2 0.5 %collective-permute-start.5 = (bf16[136,256]{1,0:T(8,128)(2,1)S(1)}, bf16[136,256]{1,0:T(8,128)(2,1)S(1)}, u32[]{:S(2)}, u32[]{:S(2)}) collective-permute-start(bf16[136,256]{1,0:T(8,128)(2,1)S(1)} %collective-permute-done.2.refs_4_), channel_id=1, source_target_pairs={{0,2},{2,0},{4,6},{6,4},{8,10},{10,8},{12,14},{14,12},{1,3},{3,1},... | collective-permute-start | bytes 208904 | tf_op jit(solution)/shard_map/ppermute | solution.py:254
  10.7 0.0 collective-permute-done.1.refs_3_
  10.7 1.5 %collective-permute-start.4 = (bf16[136,256]{1,0:T(8,128)(2,1)S(1)}, bf16[136,256]{1,0:T(8,128)(2,1)S(1)}, u32[]{:S(2)}, u32[]{:S(2)}) collective-permute-start(bf16[136,256]{1,0:T(8,128)(2,1)S(1)} %collective-permute-done.1.refs_3_), channel_id=1, source_target_pairs={{0,2},{2,0},{4,6},{6,4},{8,10},{10,8},{12,14},{14,12},{1,3},{3,1},... | collective-permute-start | bytes 208904 | tf_op jit(solution)/shard_map/ppermute | solution.py:254
  12.2 0.0 collective-permute-done.3.refs_5_
  12.2 0.5 %collective-permute-start.6 = (bf16[136,256]{1,0:T(8,128)(2,1)S(1)}, bf16[136,256]{1,0:T(8,128)(2,1)S(1)}, u32[]{:S(2)}, u32[]{:S(2)}) collective-permute-start(bf16[136,256]{1,0:T(8,128)(2,1)S(1)} %collective-permute-done.3.refs_5_), channel_id=1, source_target_pairs={{0,2},{2,0},{4,6},{6,4},{8,10},{10,8},{12,14},{14,12},{1,3},{3,1},... | collective-permute-start | bytes 208904 | tf_op jit(solution)/shard_map/ppermute | solution.py:254
  12.7 1.0 %collective-permute-done.refs_2_ = bf16[136,256]{1,0:T(8,128)(2,1)S(1)} collective-permute-done((bf16[136,256]{1,0:T(8,128)(2,1)S(1)}, bf16[136,256]{1,0:T(8,128)(2,1)S(1)}, u32[]{:S(2)}, u32[]{:S(2)}) %collective-permute-start) | collective-permute-done | bytes 69664 | tf_op jit(solution)/shard_map/ppermute | solution.py:254
  13.7 2.1 %near.1 = (bf16[1024,128]{1,0:T(8,128)(2,1)S(1)}, f32[128,128]{1,0:T(8,128)S(1)}, f32[1024,128]{1,0:T(8,128)S(1)}, f32[1024,128]{1,0:T(8,128)S(1)}, f32[1024,128]{1,0:T(8,128)S(1)}, /*index=5*/bf16[128,512]{1,0:T(8,128)(2,1)}) custom-call(bf16[128,512]{1,0:T(8,128)(2,1)} %refs_0_.1, bf16[136,256]{1,0:T(8,128)(2,1)S(1)} %pack.1.refs_1_, ...), custom_call_target="tpu_custom_call" | custom-call | tf_op jit(solution)/shard_map/near/pallas_call | solution.py:259
  15.8 0.0 collective-permute-done.5.refs_7_
  15.9 0.5 %collective-permute-done.4.refs_6_ = bf16[136,256]{1,0:T(8,128)(2,1)S(1)} collective-permute-done((bf16[136,256]{1,0:T(8,128)(2,1)S(1)}, bf16[136,256]{1,0:T(8,128)(2,1)S(1)}, u32[]{:S(2)}, u32[]{:S(2)}) %collective-permute-start.4) | collective-permute-done | bytes 69664 | tf_op jit(solution)/shard_map/ppermute | solution.py:254
  16.4 0.7 %collective-permute-done.6.refs_8_ = bf16[136,256]{1,0:T(8,128)(2,1)S(1)} collective-permute-done((bf16[136,256]{1,0:T(8,128)(2,1)S(1)}, bf16[136,256]{1,0:T(8,128)(2,1)S(1)}, u32[]{:S(2)}, u32[]{:S(2)}) %collective-permute-start.6) | collective-permute-done | bytes 69664 | tf_op jit(solution)/shard_map/ppermute | solution.py:254
  17.1 1.6 %far.1 = bf16[128,512]{1,0:T(8,128)(2,1)} custom-call(bf16[1024,128]{1,0:T(8,128)(2,1)S(1)} %get-tuple-element.11.refs_0_, f32[128,128]{1,0:T(8,128)S(1)} %get-tuple-element.12.refs_1_, f32[1024,128]{1,0:T(8,128)S(1)} %get-tuple-element.13.refs_2_, f32[1024,128]{1,0:T(8,128)S(1)} %get-tuple-element.14.refs_3_, ...), custom_call_target="tpu_custom_call", output_to_operand_aliasing={{}: (5, {})} | custom-call | tf_op jit(solution)/shard_map/far/pallas_call | solution.py:279
Async XLA Ops:
  0.8 5.9 %collective-permute-start.2 = (bf16[136,256]{1,0:T(8,128)(2,1)S(1)}, bf16[136,256]{1,0:T(8,128)(2,1)S(1)}, u32[]{:S(2)}, u32[]{:S(2)}) collective-permute-start(bf16[136,256]{1,0:T(8,128)(2,1)S(1)} %pack.1.refs_1_), channel_id=1, source_target_pairs={{0,8},{2,10},{4,12},{6,14},{8,0},{10,2},{12,4},{14,6},{1,9},{3,11}... | collective-permute-start | bytes 208904 | tf_op jit(solution)/shard_map/ppermute | solution.py:254
  0.9 9.8 %collective-permute-start.1 = (bf16[136,256]{1,0:T(8,128)(2,1)S(1)}, bf16[136,256]{1,0:T(8,128)(2,1)S(1)}, u32[]{:S(2)}, u32[]{:S(2)}) collective-permute-start(bf16[136,256]{1,0:T(8,128)(2,1)S(1)} %pack.1.refs_1_), channel_id=1, source_target_pairs={{0,4},{2,6},{4,0},{6,2},{8,12},{10,14},{12,8},{14,10},{1,5},{3,7},... | collective-permute-start | bytes 208904 | tf_op jit(solution)/shard_map/ppermute | solution.py:254
  6.7 5.5 %collective-permute-start.3 = (bf16[136,256]{1,0:T(8,128)(2,1)S(1)}, bf16[136,256]{1,0:T(8,128)(2,1)S(1)}, u32[]{:S(2)}, u32[]{:S(2)}) collective-permute-start(bf16[136,256]{1,0:T(8,128)(2,1)S(1)} %collective-permute-done.2.refs_4_), channel_id=1, source_target_pairs={{0,4},{2,6},{4,0},{6,2},{8,12},{10,14},{12,8},{14,10},{1,5},{3,7},... | collective-permute-start | bytes 208904 | tf_op jit(solution)/shard_map/ppermute | solution.py:254
  8.7 5.0 %collective-permute-start = (bf16[136,256]{1,0:T(8,128)(2,1)S(1)}, bf16[136,256]{1,0:T(8,128)(2,1)S(1)}, u32[]{:S(2)}, u32[]{:S(2)}) collective-permute-start(bf16[136,256]{1,0:T(8,128)(2,1)S(1)} %pack.1.refs_1_), channel_id=1, source_target_pairs={{0,2},{2,0},{4,6},{6,4},{8,10},{10,8},{12,14},{14,12},{1,3},{3,1},... | collective-permute-start | bytes 208904 | tf_op jit(solution)/shard_map/ppermute | solution.py:254
  10.2 5.7 %collective-permute-start.5 = (bf16[136,256]{1,0:T(8,128)(2,1)S(1)}, bf16[136,256]{1,0:T(8,128)(2,1)S(1)}, u32[]{:S(2)}, u32[]{:S(2)}) collective-permute-start(bf16[136,256]{1,0:T(8,128)(2,1)S(1)} %collective-permute-done.2.refs_4_), channel_id=1, source_target_pairs={{0,2},{2,0},{4,6},{6,4},{8,10},{10,8},{12,14},{14,12},{1,3},{3,1},... | collective-permute-start | bytes 208904 | tf_op jit(solution)/shard_map/ppermute | solution.py:254
  10.7 5.7 %collective-permute-start.4 = (bf16[136,256]{1,0:T(8,128)(2,1)S(1)}, bf16[136,256]{1,0:T(8,128)(2,1)S(1)}, u32[]{:S(2)}, u32[]{:S(2)}) collective-permute-start(bf16[136,256]{1,0:T(8,128)(2,1)S(1)} %collective-permute-done.1.refs_3_), channel_id=1, source_target_pairs={{0,2},{2,0},{4,6},{6,4},{8,10},{10,8},{12,14},{14,12},{1,3},{3,1},... | collective-permute-start | bytes 208904 | tf_op jit(solution)/shard_map/ppermute | solution.py:254
  12.2 4.9 %collective-permute-start.6 = (bf16[136,256]{1,0:T(8,128)(2,1)S(1)}, bf16[136,256]{1,0:T(8,128)(2,1)S(1)}, u32[]{:S(2)}, u32[]{:S(2)}) collective-permute-start(bf16[136,256]{1,0:T(8,128)(2,1)S(1)} %collective-permute-done.3.refs_5_), channel_id=1, source_target_pairs={{0,2},{2,0},{4,6},{6,4},{8,10},{10,8},{12,14},{14,12},{1,3},{3,1},... | collective-permute-start | bytes 208904 | tf_op jit(solution)/shard_map/ppermute | solution.py:254

commit v2 on v1

--- a/solution.py
+++ b/solution.py
@@ -120,20 +120,33 @@
         after(head, rows, top, total, mixed)
 
 
-def assemble(results, repeat, width, lanes, out_buf):
-    tokens = out_buf.shape[0]
-    lane = lax.broadcasted_iota(jnp.int32, (tokens, lanes), 1)
-    per_tile = lanes // width
-    for tile in range(len(results) // per_tile):
-        whole = None
-        for slot in range(per_tile):
-            head = tile * per_tile + slot
-            shift = (slot * width - head // repeat * width) % lanes
-            value = results[head]
-            if shift:
-                value = pltpu.roll(value, shift, 1)
-            whole = value if whole is None else jnp.where(lane >= slot * width, value, whole)
-        out_buf[:, tile * lanes : (tile + 1) * lanes] = whole.astype(jnp.bfloat16)
+class Output:
+    def __init__(self, repeat, width, lanes, buf, hbm, sems):
+        self.repeat, self.width, self.lanes = repeat, width, lanes
+        self.buf, self.hbm, self.sems = buf, hbm, sems
+        self.head, self.whole, self.copies = 0, None, []
+
+    def add(self, value):
+        slot = self.head % (self.lanes // self.width)
+        shift = (slot * self.width - self.head // self.repeat * self.width) % self.lanes
+        if shift:
+            value = pltpu.roll(value, shift, 1)
+        if slot:
+            lane = lax.broadcasted_iota(jnp.int32, value.shape, 1)
+            value = jnp.where(lane >= slot * self.width, value, self.whole)
+        self.whole = value
+        self.head += 1
+        if (slot + 1) * self.width == self.lanes:
+            tile = len(self.copies)
+            where = slice(tile * self.lanes, (tile + 1) * self.lanes)
+            self.buf[:, where] = value.astype(jnp.bfloat16)
+            copy = pltpu.make_async_copy(self.buf.at[:, where], self.hbm.at[:, where], self.sems.at[tile])
+            copy.start()
+            self.copies.append(copy)
+
+    def finish(self):
+        for copy in self.copies:
+            copy.wait()
 
 
 def normal(total, mixed):
@@ -148,26 +161,23 @@
     return [step for step in range(2, count, 2) if pair ^ (step >> 1) < pair]
 
 
-def near_kernel(groups, repeat, count, *refs):
-    steps = [0, 1] + list(range(2, count, 2))
-    q_hbm, pieces = refs[0], dict(zip(steps, refs[1 : 1 + len(steps)]))
-    q_all, seg_ref, top_ref, sum_ref, mix_ref, out_hbm, q_buf, scores, sem = refs[1 + len(steps) :]
-    tokens, _ = q_buf.shape
+def prep_kernel(groups, repeat, q_hbm, own, q_all, seg_ref, q_buf, sems):
+    tokens, columns = q_buf.shape
     lanes = q_all.shape[1]
     width = lanes // groups
-    heads = groups * repeat
-    factor = math.log2(math.e) / math.sqrt(width)
-    me = lax.axis_index("seq")
-
-    copy = pltpu.make_async_copy(q_hbm, q_buf, sem)
-    copy.start()
-    query_seg = jnp.transpose(seg_grid(pieces[0], tokens))
-    seg_ref[...] = query_seg
+    copies = [
+        pltpu.make_async_copy(q_hbm.at[:, at : at + lanes], q_buf.at[:, at : at + lanes], sems.at[at // lanes])
+        for at in range(0, columns, lanes)
+    ]
+    for copy in copies:
+        copy.start()
+    seg_ref[...] = jnp.transpose(seg_grid(own, tokens))
     lane = lax.broadcasted_iota(jnp.int32, (tokens, lanes), 1)
-    copy.wait()
-    for head in range(heads):
+    for head in range(groups * repeat):
         group = head // repeat
         first = head * width // lanes * lanes
+        if first == head * width:
+            copies[first // lanes].wait()
         tile = q_buf[:, first : first + lanes].astype(jnp.float32)
         shift = (group * width - (head * width - first)) % lanes
         if shift:
@@ -175,6 +185,19 @@
         keep = (lane >= group * width) & (lane < (group + 1) * width)
         q_all[head * tokens : (head + 1) * tokens, :] = jnp.where(keep, tile, 0.0).astype(jnp.bfloat16)
 
+
+def near_kernel(groups, repeat, count, *refs):
+    steps = [0, 1] + list(range(2, count, 2))
+    q_all, seg_ref, pieces = refs[0], refs[1], dict(zip(steps, refs[2 : 2 + len(steps)]))
+    top_ref, sum_ref, mix_ref, out_hbm, out_buf, scores, sems = refs[2 + len(steps) :]
+    lanes = q_all.shape[1]
+    tokens = seg_ref.shape[0]
+    width = lanes // groups
+    heads = groups * repeat
+    factor = math.log2(math.e) / math.sqrt(width)
+    me = lax.axis_index("seq")
+    query_seg = seg_ref[...]
+
     for pair in range(count // 2):
 
         @pl.when(me // 2 == pair)
@@ -182,7 +205,7 @@
             early = seen_steps(pair, count)
             chosen = [0, 1] + early[len(early) % 2 :] + early[: len(early) % 2]
             blocks = paired([(step, pieces[step]) for step in chosen])
-            results = []
+            output = Output(repeat, width, lanes, out_buf, out_hbm, sems)
 
             def after(head, rows, top, total, mixed):
                 if early:
@@ -190,21 +213,17 @@
                     sum_ref[rows, :] = total
                     mix_ref[rows, :] = mixed
                 else:
-                    results.append(normal(total, mixed))
+                    output.add(normal(total, mixed))
 
             attend(me, blocks, query_seg, q_all, scores, heads, factor, lanes, lambda rows: None, after)
-            if not early:
-                assemble(results, repeat, width, lanes, q_buf)
-                out_copy = pltpu.make_async_copy(q_buf, out_hbm, sem)
-                out_copy.start()
-                out_copy.wait()
+            output.finish()
 
 
 def far_kernel(groups, repeat, count, *refs):
     steps = list(range(3, count, 2))
     q_all, seg_ref, top_ref, sum_ref, mix_ref, out_in = refs[:6]
     pieces = dict(zip(steps, refs[6 : 6 + len(steps)]))
-    out_hbm, out_buf, scores, sem = refs[6 + len(steps) :]
+    out_hbm, out_buf, scores, sems = refs[6 + len(steps) :]
     del out_in
     lanes = q_all.shape[1]
     width = lanes // groups
@@ -217,30 +236,21 @@
         @pl.when(me // 2 == pair)
         def _(pair=pair):
             blocks = paired([(step + 1, pieces[step + 1]) for step in seen_steps(pair, count)])
-            results = []
+            output = Output(repeat, width, lanes, out_buf, out_hbm, sems)
 
             def before(rows):
                 return top_ref[rows, :], sum_ref[rows, :], mix_ref[rows, :]
 
             def after(head, rows, top, total, mixed):
-                results.append(normal(total, mixed))
+                output.add(normal(total, mixed))
 
             attend(me, blocks, seg_ref[...], q_all, scores, heads, factor, lanes, before, after)
-            assemble(results, repeat, width, lanes, out_buf)
-            out_copy = pltpu.make_async_copy(out_buf, out_hbm, sem)
-            out_copy.start()
-            out_copy.wait()
+            output.finish()
 
 
 def plan_of(count):
-    powers = [1 << bit for bit in range(1, count.bit_length() - 1)]
-    plan = [(step, 0, step) for step in reversed(powers)] + [(1, 0, 1)]
-    for step in range(2, count, 2):
-        if step not in powers:
-            low = step & -step
-            plan.append((step, step ^ low, low))
-    plan += [(step + 1, step, 1) for step in range(2, count, 2)]
-    return plan
+    column = [count - 2] + list(range(2, count - 2, 2))
+    return [(step, 0, step) for step in column] + [(1, 0, 1)] + [(step + 1, step, 1) for step in column]
 
 
 def per_device(count, queries, key_matrix, value_matrix, segment_ids):
@@ -256,26 +266,40 @@
     far = list(range(3, count, 2))
     row_shape = (heads * tokens, lanes)
     score_shape = (heads * tokens, 2 * tokens)
-    *state, out = pl.pallas_call(
-        functools.partial(near_kernel, groups, repeat, count),
+    tiles = queries.shape[1] // lanes
+    q_all, query_seg = pl.pallas_call(
+        functools.partial(prep_kernel, groups, repeat),
         out_shape=[
             pltpu.VMEM(row_shape, jnp.bfloat16),
             pltpu.VMEM((tokens, tokens), jnp.float32),
+        ],
+        in_specs=[HBM, VMEM],
+        out_specs=[VMEM] * 2,
+        scratch_shapes=[
+            pltpu.VMEM(queries.shape, queries.dtype),
+            pltpu.SemaphoreType.DMA((tiles,)),
+        ],
+        compiler_params=pltpu.CompilerParams(vmem_limit_bytes=SMALL_VMEM),
+        name="prep",
+    )(in_hbm(queries), held[0])
+    top, total, mixed, out = pl.pallas_call(
+        functools.partial(near_kernel, groups, repeat, count),
+        out_shape=[
             pltpu.VMEM(row_shape, jnp.float32),
             pltpu.VMEM(row_shape, jnp.float32),
             pltpu.VMEM(row_shape, jnp.float32),
             pltpu.HBM(queries.shape, queries.dtype),
         ],
-        in_specs=[HBM] + [VMEM] * len(near),
-        out_specs=[VMEM] * 5 + [HBM],
+        in_specs=[VMEM] * (2 + len(near)),
+        out_specs=[VMEM] * 3 + [HBM],
         scratch_shapes=[
             pltpu.VMEM(queries.shape, queries.dtype),
             pltpu.VMEM(((len(near) + 1) // 2,) + score_shape, jnp.float32),
-            pltpu.SemaphoreType.DMA,
+            pltpu.SemaphoreType.DMA((tiles,)),
         ],
         compiler_params=pltpu.CompilerParams(vmem_limit_bytes=VMEM_LIMIT),
         name="near",
-    )(in_hbm(queries), *[held[step] for step in near])
+    )(q_all, query_seg, *[held[step] for step in near])
     return pl.pallas_call(
         functools.partial(far_kernel, groups, repeat, count),
         out_shape=pltpu.HBM(queries.shape, queries.dtype),
@@ -284,12 +308,12 @@
         scratch_shapes=[
             pltpu.VMEM(queries.shape, queries.dtype),
             pltpu.VMEM(((len(far) + 1) // 2,) + score_shape, jnp.float32),
-            pltpu.SemaphoreType.DMA,
+            pltpu.SemaphoreType.DMA((tiles,)),
         ],
         input_output_aliases={5: 0},
         compiler_params=pltpu.CompilerParams(vmem_limit_bytes=VMEM_LIMIT),
         name="far",
-    )(*state, out, *[held[step] for step in far])
+    )(q_all, query_seg, top, total, mixed, out, *[held[step] for step in far])
 
 
 def attend_block(state, query_heads, query_pos, query_seg, key_blk, value_blk, seg_blk, key_start):

time: 18.9 us -> 17.6 us (0.931)
  the two profiles are of different devices: /device:TPU:16 before, /device:TPU:0 now
where the time goes in v2:
time: 17.6 us; the launch traced here: 17.3 us
  starting transfers between devices  10.5 us (60%)
  Pallas kernels  3.53 us (20%)
  waiting for transfers between devices  3.23 us (18%)
    ppermute x7, starting transfers between devices, per_device(): lax.ppermute(held[source], 'seq', [(i, i ^ mask) for i in range(count)])  10.5 us
    ppermute x7, waiting for transfers between devices, per_device(): lax.ppermute(held[source], 'seq', [(i, i ^ mask) for i in range(count)])  3.23 us
    pallas_call x1, Pallas kernels, per_device(): pl.pallas_call(functools.partial(near_kernel, groups, repeat, count), out...  1.55 us
    pallas_call x1, Pallas kernels, per_device(): pl.pallas_call(functools.partial(prep_kernel, groups, repeat), out_shape=...  1.12 us
    pallas_call x1, Pallas kernels, pack(): pl.pallas_call(pack_kernel, out_shape=pltpu.VMEM((tokens + SEG_ROWS, 2 *...  0.81 us
  transfers between devices with their start and end apart: 7, of which 2 were waited for; matrix products, arithmetic and copies ran while one was open for 0% of the time, Pallas kernels for 15%

profile of v2, /device:TPU:0, one launch (start us, length us, event | category | flops | bytes accessed | tf_op | source)
XLA Modules:
  0.0 17.3 jit_solution(10977306206790427732)
XLA Ops:
  0.0 0.8 %pack.1.own.refs_2_ = bf16[136,256]{1,0:T(8,128)(2,1)S(1)} custom-call(bf16[128,128]{1,0:T(8,128)(2,1)} %k_ref.1, bf16[128,128]{1,0:T(8,128)(2,1)} %v_ref.1, s32[1,128]{1,0:T(1,128)} %bitcast.1), custom_call_target="tpu_custom_call" | custom-call | tf_op jit(solution)/shard_map/pack/pallas_call | solution.py:44
  0.8 3.1 %collective-permute-start.1 = (bf16[136,256]{1,0:T(8,128)(2,1)S(1)}, bf16[136,256]{1,0:T(8,128)(2,1)S(1)}, u32[]{:S(2)}, u32[]{:S(2)}) collective-permute-start(bf16[136,256]{1,0:T(8,128)(2,1)S(1)} %pack.1.own.refs_2_), channel_id=1, source_target_pairs={{0,4},{2,6},{4,0},{6,2},{8,12},{10,14},{12,8},{14,10},{1,5},{3,7},... | collective-permute-start | bytes 208904 | tf_op jit(solution)/shard_map/ppermute | solution.py:264
  3.9 2.6 %collective-permute-start.2 = (bf16[136,256]{1,0:T(8,128)(2,1)S(1)}, bf16[136,256]{1,0:T(8,128)(2,1)S(1)}, u32[]{:S(2)}, u32[]{:S(2)}) collective-permute-start(bf16[136,256]{1,0:T(8,128)(2,1)S(1)} %pack.1.own.refs_2_), channel_id=1, source_target_pairs={{0,8},{2,10},{4,12},{6,14},{8,0},{10,2},{12,4},{14,6},{1,9},{3,11}... | collective-permute-start | bytes 208904 | tf_op jit(solution)/shard_map/ppermute | solution.py:264
  6.5 0.0 collective-permute-start.3
  6.5 1.7 %collective-permute-start = (bf16[136,256]{1,0:T(8,128)(2,1)S(1)}, bf16[136,256]{1,0:T(8,128)(2,1)S(1)}, u32[]{:S(2)}, u32[]{:S(2)}) collective-permute-start(bf16[136,256]{1,0:T(8,128)(2,1)S(1)} %pack.1.own.refs_2_), channel_id=1, source_target_pairs={{0,2},{2,0},{4,6},{6,4},{8,10},{10,8},{12,14},{14,12},{1,3},{3,1},... | collective-permute-start | bytes 208904 | tf_op jit(solution)/shard_map/ppermute | solution.py:264
  8.2 0.0 collective-permute-done.1.refs_4_
  8.2 0.3 %collective-permute-start.4 = (bf16[136,256]{1,0:T(8,128)(2,1)S(1)}, bf16[136,256]{1,0:T(8,128)(2,1)S(1)}, u32[]{:S(2)}, u32[]{:S(2)}) collective-permute-start(bf16[136,256]{1,0:T(8,128)(2,1)S(1)} %collective-permute-done.1.refs_4_), channel_id=1, source_target_pairs={{0,2},{2,0},{4,6},{6,4},{8,10},{10,8},{12,14},{14,12},{1,3},{3,1},... | collective-permute-start | bytes 208904 | tf_op jit(solution)/shard_map/ppermute | solution.py:264
  8.6 2.9 %collective-permute-done.2.refs_5_ = bf16[136,256]{1,0:T(8,128)(2,1)S(1)} collective-permute-done((bf16[136,256]{1,0:T(8,128)(2,1)S(1)}, bf16[136,256]{1,0:T(8,128)(2,1)S(1)}, u32[]{:S(2)}, u32[]{:S(2)}) %collective-permute-start.2) | collective-permute-done | bytes 69664 | tf_op jit(solution)/shard_map/ppermute | solution.py:264
  11.5 1.5 %collective-permute-start.5 = (bf16[136,256]{1,0:T(8,128)(2,1)S(1)}, bf16[136,256]{1,0:T(8,128)(2,1)S(1)}, u32[]{:S(2)}, u32[]{:S(2)}) collective-permute-start(bf16[136,256]{1,0:T(8,128)(2,1)S(1)} %collective-permute-done.2.refs_5_), channel_id=1, source_target_pairs={{0,2},{2,0},{4,6},{6,4},{8,10},{10,8},{12,14},{14,12},{1,3},{3,1},... | collective-permute-start | bytes 208904 | tf_op jit(solution)/shard_map/ppermute | solution.py:264
  13.0 0.0 collective-permute-done.3.refs_6_
  13.0 1.3 %collective-permute-start.6 = (bf16[136,256]{1,0:T(8,128)(2,1)S(1)}, bf16[136,256]{1,0:T(8,128)(2,1)S(1)}, u32[]{:S(2)}, u32[]{:S(2)}) collective-permute-start(bf16[136,256]{1,0:T(8,128)(2,1)S(1)} %collective-permute-done.3.refs_6_), channel_id=1, source_target_pairs={{0,2},{2,0},{4,6},{6,4},{8,10},{10,8},{12,14},{14,12},{1,3},{3,1},... | collective-permute-start | bytes 208904 | tf_op jit(solution)/shard_map/ppermute | solution.py:264
  14.2 1.1 %prep.1 = (bf16[1024,128]{1,0:T(8,128)(2,1)S(1)}, f32[128,128]{1,0:T(8,128)S(1)}) custom-call(bf16[128,512]{1,0:T(8,128)(2,1)} %q_hbm.1, bf16[136,256]{1,0:T(8,128)(2,1)S(1)} %pack.1.own.refs_2_), custom_call_target="tpu_custom_call" | custom-call | tf_op jit(solution)/shard_map/prep/pallas_call | solution.py:270
  15.4 0.0 collective-permute-done.refs_3_
  15.4 1.6 %near.1 = (f32[1024,128]{1,0:T(8,128)S(1)}, f32[1024,128]{1,0:T(8,128)S(1)}, f32[1024,128]{1,0:T(8,128)S(1)}, bf16[128,512]{1,0:T(8,128)(2,1)}) custom-call(bf16[1024,128]{1,0:T(8,128)(2,1)S(1)} %get-tuple-element.11.refs_0_, f32[128,128]{1,0:T(8,128)S(1)} %get-tuple-element.12.refs_1_, bf16[136,256]{1,0:T(8,128)(2,1)S(1)} %pack.1.own.refs_2_, ...), custom_call_target="tpu_custom_call" | custom-call | tf_op jit(solution)/shard_map/near/pallas_call | solution.py:285
  16.9 0.0 collective-permute-done.4.refs_6_
  16.9 0.0 collective-permute-done.5.refs_7_
  17.0 0.3 %collective-permute-done.6.refs_8_ = bf16[136,256]{1,0:T(8,128)(2,1)S(1)} collective-permute-done((bf16[136,256]{1,0:T(8,128)(2,1)S(1)}, bf16[136,256]{1,0:T(8,128)(2,1)S(1)}, u32[]{:S(2)}, u32[]{:S(2)}) %collective-permute-start.6) | collective-permute-done | bytes 69664 | tf_op jit(solution)/shard_map/ppermute | solution.py:264
  (1 shorter events, 0.0 us)
Async XLA Ops:
  0.8 7.4 %collective-permute-start.1 = (bf16[136,256]{1,0:T(8,128)(2,1)S(1)}, bf16[136,256]{1,0:T(8,128)(2,1)S(1)}, u32[]{:S(2)}, u32[]{:S(2)}) collective-permute-start(bf16[136,256]{1,0:T(8,128)(2,1)S(1)} %pack.1.own.refs_2_), channel_id=1, source_target_pairs={{0,4},{2,6},{4,0},{6,2},{8,12},{10,14},{12,8},{14,10},{1,5},{3,7},... | collective-permute-start | bytes 208904 | tf_op jit(solution)/shard_map/ppermute | solution.py:264
  3.9 7.5 %collective-permute-start.2 = (bf16[136,256]{1,0:T(8,128)(2,1)S(1)}, bf16[136,256]{1,0:T(8,128)(2,1)S(1)}, u32[]{:S(2)}, u32[]{:S(2)}) collective-permute-start(bf16[136,256]{1,0:T(8,128)(2,1)S(1)} %pack.1.own.refs_2_), channel_id=1, source_target_pairs={{0,8},{2,10},{4,12},{6,14},{8,0},{10,2},{12,4},{14,6},{1,9},{3,11}... | collective-permute-start | bytes 208904 | tf_op jit(solution)/shard_map/ppermute | solution.py:264
  6.5 6.4 %collective-permute-start.3 = (bf16[136,256]{1,0:T(8,128)(2,1)S(1)}, bf16[136,256]{1,0:T(8,128)(2,1)S(1)}, u32[]{:S(2)}, u32[]{:S(2)}) collective-permute-start(bf16[136,256]{1,0:T(8,128)(2,1)S(1)} %pack.1.own.refs_2_), channel_id=1, source_target_pairs={{0,12},{2,14},{4,8},{6,10},{8,4},{10,6},{12,0},{14,2},{1,13},{3,15... | collective-permute-start | bytes 208904 | tf_op jit(solution)/shard_map/ppermute | solution.py:264
  6.5 8.8 %collective-permute-start = (bf16[136,256]{1,0:T(8,128)(2,1)S(1)}, bf16[136,256]{1,0:T(8,128)(2,1)S(1)}, u32[]{:S(2)}, u32[]{:S(2)}) collective-permute-start(bf16[136,256]{1,0:T(8,128)(2,1)S(1)} %pack.1.own.refs_2_), channel_id=1, source_target_pairs={{0,2},{2,0},{4,6},{6,4},{8,10},{10,8},{12,14},{14,12},{1,3},{3,1},... | collective-permute-start | bytes 208904 | tf_op jit(solution)/shard_map/ppermute | solution.py:264
  8.2 8.7 %collective-permute-start.4 = (bf16[136,256]{1,0:T(8,128)(2,1)S(1)}, bf16[136,256]{1,0:T(8,128)(2,1)S(1)}, u32[]{:S(2)}, u32[]{:S(2)}) collective-permute-start(bf16[136,256]{1,0:T(8,128)(2,1)S(1)} %collective-permute-done.1.refs_4_), channel_id=1, source_target_pairs={{0,2},{2,0},{4,6},{6,4},{8,10},{10,8},{12,14},{14,12},{1,3},{3,1},... | collective-permute-start | bytes 208904 | tf_op jit(solution)/shard_map/ppermute | solution.py:264
  11.5 5.5 %collective-permute-start.5 = (bf16[136,256]{1,0:T(8,128)(2,1)S(1)}, bf16[136,256]{1,0:T(8,128)(2,1)S(1)}, u32[]{:S(2)}, u32[]{:S(2)}) collective-permute-start(bf16[136,256]{1,0:T(8,128)(2,1)S(1)} %collective-permute-done.2.refs_5_), channel_id=1, source_target_pairs={{0,2},{2,0},{4,6},{6,4},{8,10},{10,8},{12,14},{14,12},{1,3},{3,1},... | collective-permute-start | bytes 208904 | tf_op jit(solution)/shard_map/ppermute | solution.py:264
  13.0 4.3 %collective-permute-start.6 = (bf16[136,256]{1,0:T(8,128)(2,1)S(1)}, bf16[136,256]{1,0:T(8,128)(2,1)S(1)}, u32[]{:S(2)}, u32[]{:S(2)}) collective-permute-start(bf16[136,256]{1,0:T(8,128)(2,1)S(1)} %collective-permute-done.3.refs_6_), channel_id=1, source_target_pairs={{0,2},{2,0},{4,6},{6,4},{8,10},{10,8},{12,14},{14,12},{1,3},{3,1},... | collective-permute-start | bytes 208904 | tf_op jit(solution)/shard_map/ppermute | solution.py:264

commit v3 on v2

--- a/solution.py
+++ b/solution.py
@@ -23,18 +23,17 @@
 
 
 def pack_kernel(k_ref, v_ref, seg_ref, out_ref, seg_buf, sems):
-    tokens, lanes = k_ref.shape
+    tokens = k_ref.shape[0]
     copies = [
         pltpu.make_async_copy(seg_ref, seg_buf, sems.at[0]),
-        pltpu.make_async_copy(k_ref, out_ref.at[:tokens, :lanes], sems.at[1]),
-        pltpu.make_async_copy(v_ref, out_ref.at[:tokens, lanes:], sems.at[2]),
+        pltpu.make_async_copy(k_ref, out_ref.at[:tokens], sems.at[1]),
+        pltpu.make_async_copy(v_ref, out_ref.at[tokens : 2 * tokens], sems.at[2]),
     ]
     for copy in copies:
         copy.start()
     copies[0].wait()
-    row = jnp.broadcast_to(seg_buf[...].astype(jnp.float32), (SEG_ROWS, tokens)).astype(jnp.bfloat16)
-    out_ref[tokens:, :lanes] = row
-    out_ref[tokens:, lanes:] = row
+    row = jnp.broadcast_to(seg_buf[...].astype(jnp.float32), (SEG_ROWS, tokens))
+    out_ref[2 * tokens :] = row.astype(jnp.bfloat16)
     copies[1].wait()
     copies[2].wait()
 
@@ -43,7 +42,7 @@
     tokens, lanes = key_matrix.shape
     return pl.pallas_call(
         pack_kernel,
-        out_shape=pltpu.VMEM((tokens + SEG_ROWS, 2 * lanes), key_matrix.dtype),
+        out_shape=pltpu.VMEM((2 * tokens + SEG_ROWS, lanes), key_matrix.dtype),
         in_specs=[HBM] * 3,
         out_specs=VMEM,
         scratch_shapes=[pltpu.VMEM((1, tokens), jnp.int32), pltpu.SemaphoreType.DMA((3,))],
@@ -52,13 +51,13 @@
     )(in_hbm(key_matrix), in_hbm(value_matrix), in_hbm(seg_row))
 
 
-def joined(pieces, first, width, tokens):
-    parts = [piece[:tokens, first : first + width] for piece in pieces]
+def joined(pieces, first, tokens):
+    parts = [piece[first : first + tokens] for piece in pieces]
     return parts[0] if len(parts) == 1 else jnp.concatenate(parts, axis=0)
 
 
 def seg_grid(piece, tokens):
-    line = piece[tokens : tokens + SEG_ROWS, :tokens].astype(jnp.float32)[0:1]
+    line = piece[2 * tokens :].astype(jnp.float32)[0:1]
     return jnp.broadcast_to(line, (tokens, tokens))
 
 
@@ -81,19 +80,19 @@
     return functools.reduce(op, parts)
 
 
-def attend(me, blocks, query_seg, q_all, scores, heads, factor, lanes, before, after):
+def attend(me, blocks, query_seg, q_all, scores, heads, factor, before, after):
     tokens = query_seg.shape[0]
     query_rows = q_all[...]
     biases, value_blocks = [], []
     for number, block in enumerate(blocks):
         members = [piece for _, piece in block]
         scores[number, :, : len(block) * tokens] = lax.dot_general(
-            query_rows, joined(members, 0, lanes, tokens), (((1,), (1,)), ((), ())),
+            query_rows, joined(members, 0, tokens), (((1,), (1,)), ((), ())),
             preferred_element_type=jnp.float32,
         )
         parts = [bias_of(me, step, piece, query_seg) for step, piece in block]
         biases.append(parts[0] if len(parts) == 1 else jnp.concatenate(parts, axis=1))
-        value_blocks.append(joined(members, lanes, lanes, tokens))
+        value_blocks.append(joined(members, tokens, tokens))
     for head in range(heads):
         rows = slice(head * tokens, (head + 1) * tokens)
         state = before(rows)
@@ -186,8 +185,16 @@
         q_all[head * tokens : (head + 1) * tokens, :] = jnp.where(keep, tile, 0.0).astype(jnp.bfloat16)
 
 
+def near_steps(count):
+    return [0, 1] + list(range(2, count, 2)) + [count - 1]
+
+
+def far_steps(count):
+    return list(range(3, count - 1, 2))
+
+
 def near_kernel(groups, repeat, count, *refs):
-    steps = [0, 1] + list(range(2, count, 2))
+    steps = near_steps(count)
     q_all, seg_ref, pieces = refs[0], refs[1], dict(zip(steps, refs[2 : 2 + len(steps)]))
     top_ref, sum_ref, mix_ref, out_hbm, out_buf, scores, sems = refs[2 + len(steps) :]
     lanes = q_all.shape[1]
@@ -203,7 +210,7 @@
         @pl.when(me // 2 == pair)
         def _(pair=pair):
             early = seen_steps(pair, count)
-            chosen = [0, 1] + early[len(early) % 2 :] + early[: len(early) % 2]
+            chosen = [step for step in steps if step < 2 or step & -2 in early]
             blocks = paired([(step, pieces[step]) for step in chosen])
             output = Output(repeat, width, lanes, out_buf, out_hbm, sems)
 
@@ -215,12 +222,12 @@
                 else:
                     output.add(normal(total, mixed))
 
-            attend(me, blocks, query_seg, q_all, scores, heads, factor, lanes, lambda rows: None, after)
+            attend(me, blocks, query_seg, q_all, scores, heads, factor, lambda rows: None, after)
             output.finish()
 
 
 def far_kernel(groups, repeat, count, *refs):
-    steps = list(range(3, count, 2))
+    steps = far_steps(count)
     q_all, seg_ref, top_ref, sum_ref, mix_ref, out_in = refs[:6]
     pieces = dict(zip(steps, refs[6 : 6 + len(steps)]))
     out_hbm, out_buf, scores, sems = refs[6 + len(steps) :]
@@ -235,7 +242,8 @@
 
         @pl.when(me // 2 == pair)
         def _(pair=pair):
-            blocks = paired([(step + 1, pieces[step + 1]) for step in seen_steps(pair, count)])
+            early = seen_steps(pair, count)
+            blocks = paired([(step, pieces[step]) for step in steps if step & -2 in early])
             output = Output(repeat, width, lanes, out_buf, out_hbm, sems)
 
             def before(rows):
@@ -244,8 +252,21 @@
             def after(head, rows, top, total, mixed):
                 output.add(normal(total, mixed))
 
-            attend(me, blocks, seg_ref[...], q_all, scores, heads, factor, lanes, before, after)
+            attend(me, blocks, seg_ref[...], q_all, scores, heads, factor, before, after)
             output.finish()
+
+
+def partners(count, cores, step, mask):
+    def needs(i):
+        return step < 2 or step % 2 == 0 or (i ^ step) // 2 < i // 2
+
+    pairs = []
+    for i in range(count):
+        for core in range(cores):
+            across = needs(i) or needs(i ^ mask)
+            other = (i ^ mask) * cores + core if across else i * cores + (core ^ 1)
+            pairs.append((i * cores + core, other))
+    return pairs
 
 
 def plan_of(count):
@@ -253,7 +274,7 @@
     return [(step, 0, step) for step in column] + [(1, 0, 1)] + [(step + 1, step, 1) for step in column]
 
 
-def per_device(count, queries, key_matrix, value_matrix, segment_ids):
+def per_device(count, cores, queries, key_matrix, value_matrix, segment_ids):
     tokens, lanes = key_matrix.shape
     groups = lanes // HEAD_WIDTH
     repeat = queries.shape[1] // HEAD_WIDTH // groups
@@ -261,9 +282,9 @@
     plan = plan_of(count)
     held = {0: pack(key_matrix, value_matrix, segment_ids.reshape(1, tokens))}
     for step, source, mask in plan:
-        held[step] = lax.ppermute(held[source], "seq", [(i, i ^ mask) for i in range(count)])
-    near = [0, 1] + list(range(2, count, 2))
-    far = list(range(3, count, 2))
+        held[step] = lax.ppermute(held[source], ("seq", "head"), partners(count, cores, step, mask))
+    near = near_steps(count)
+    far = far_steps(count)
     row_shape = (heads * tokens, lanes)
     score_shape = (heads * tokens, 2 * tokens)
     tiles = queries.shape[1] // lanes
@@ -439,18 +460,19 @@
     return 8 <= count <= 16 and count & (count - 1) == 0
 
 
-def suits(count, queries, key_matrix):
+def suits(count, cores, queries, key_matrix):
     tokens, lanes = key_matrix.shape
     return (
         paired_axis(count)
+        and cores == 2
         and tokens == lanes == 2 * HEAD_WIDTH
         and queries.shape[1] % lanes == 0
     )
 
 
-def per_device_any(count, queries, key_matrix, value_matrix, segment_ids):
-    body = functools.partial(per_device, count)
-    if not suits(count, queries, key_matrix):
+def per_device_any(count, cores, queries, key_matrix, value_matrix, segment_ids):
+    body = functools.partial(per_device, count, cores)
+    if not suits(count, cores, queries, key_matrix):
         body = per_device_general
     return body(queries, key_matrix, value_matrix, segment_ids)
 
@@ -459,6 +481,6 @@
     count = mesh.shape["seq"]
     in_specs = (P(("sweep", "seq"), "head"),) * 3 + (P(("sweep", "seq")),)
     return jax.shard_map(
-        functools.partial(per_device_any, count),
+        functools.partial(per_device_any, count, mesh.shape["head"]),
         mesh=mesh, in_specs=in_specs, out_specs=P(("sweep", "seq"), "head"), check_vma=False,
     )

time: 17.6 us -> 16.1 us (0.915)
  the two profiles are of different devices: /device:TPU:0 before, /device:TPU:24 now
where the time goes in v3:
time: 16.1 us; the launch traced here: 15.8 us
  starting transfers between devices  9.45 us (59%)
  Pallas kernels  5.31 us (33%)
  waiting for transfers between devices  0.99 us (6%)
    ppermute x7, starting transfers between devices, per_device(): lax.ppermute(held[source], ('seq', 'head'), partners(count, cores, step,...  9.45 us
    pallas_call x1, Pallas kernels, per_device(): pl.pallas_call(functools.partial(near_kernel, groups, repeat, count), out...  1.76 us
    pallas_call x1, Pallas kernels, per_device(): pl.pallas_call(functools.partial(far_kernel, groups, repeat, count), out_...  1.61 us
    pallas_call x1, Pallas kernels, per_device(): pl.pallas_call(functools.partial(prep_kernel, groups, repeat), out_shape=...  1.12 us
    ppermute x7, waiting for transfers between devices, per_device(): lax.ppermute(held[source], ('seq', 'head'), partners(count, cores, step,...  0.99 us
    pallas_call x1, Pallas kernels, pack(): pl.pallas_call(pack_kernel, out_shape=pltpu.VMEM((2 * tokens + SEG_ROWS,...  0.81 us
  transfers between devices with their start and end apart: 7, of which 1 were waited for; matrix products, arithmetic and copies ran while one was open for 0% of the time, Pallas kernels for 18%

profile of v3, /device:TPU:24, one launch (start us, length us, event | category | flops | bytes accessed | tf_op | source)
XLA Modules:
  0.0 15.8 jit_solution(1603715266199581560)
XLA Ops:
  0.0 0.8 %pack.1.own.refs_2_ = bf16[264,128]{1,0:T(8,128)(2,1)S(1)} custom-call(bf16[128,128]{1,0:T(8,128)(2,1)} %k_ref.1, bf16[128,128]{1,0:T(8,128)(2,1)} %v_ref.1, s32[1,128]{1,0:T(1,128)} %bitcast.1), custom_call_target="tpu_custom_call" | custom-call | tf_op jit(solution)/shard_map/pack/pallas_call | solution.py:43
  0.8 0.1 collective-permute-start.3
  0.9 0.9 %collective-permute-start.1 = (bf16[264,128]{1,0:T(8,128)(2,1)S(1)}, bf16[264,128]{1,0:T(8,128)(2,1)S(1)}, u32[]{:S(2)}, u32[]{:S(2)}) collective-permute-start(bf16[264,128]{1,0:T(8,128)(2,1)S(1)} %pack.1.own.refs_2_), channel_id=1, source_target_pairs={{0,4},{1,5},{2,6},{3,7},{4,0},{5,1},{6,2},{7,3},{8,12},{9,13},{10,... | collective-permute-start | bytes 202760 | tf_op jit(solution)/shard_map/ppermute | solution.py:285
  1.8 3.5 %collective-permute-start.2 = (bf16[264,128]{1,0:T(8,128)(2,1)S(1)}, bf16[264,128]{1,0:T(8,128)(2,1)S(1)}, u32[]{:S(2)}, u32[]{:S(2)}) collective-permute-start(bf16[264,128]{1,0:T(8,128)(2,1)S(1)} %pack.1.own.refs_2_), channel_id=1, source_target_pairs={{0,8},{1,9},{2,10},{3,11},{4,12},{5,13},{6,14},{7,15},{8,0},{9,1},... | collective-permute-start | bytes 202760 | tf_op jit(solution)/shard_map/ppermute | solution.py:285
  5.3 1.5 %collective-permute-start = (bf16[264,128]{1,0:T(8,128)(2,1)S(1)}, bf16[264,128]{1,0:T(8,128)(2,1)S(1)}, u32[]{:S(2)}, u32[]{:S(2)}) collective-permute-start(bf16[264,128]{1,0:T(8,128)(2,1)S(1)} %pack.1.own.refs_2_), channel_id=1, source_target_pairs={{0,2},{1,3},{2,0},{3,1},{4,6},{5,7},{6,4},{7,5},{8,10},{9,11},{10,... | collective-permute-start | bytes 202760 | tf_op jit(solution)/shard_map/ppermute | solution.py:285
  6.8 0.9 %collective-permute-done.3.refs_6_ = bf16[264,128]{1,0:T(8,128)(2,1)S(1)} collective-permute-done((bf16[264,128]{1,0:T(8,128)(2,1)S(1)}, bf16[264,128]{1,0:T(8,128)(2,1)S(1)}, u32[]{:S(2)}, u32[]{:S(2)}) %collective-permute-start.3) | collective-permute-done | bytes 67616 | tf_op jit(solution)/shard_map/ppermute | solution.py:285
  7.7 1.5 %collective-permute-start.4 = (bf16[264,128]{1,0:T(8,128)(2,1)S(1)}, bf16[264,128]{1,0:T(8,128)(2,1)S(1)}, u32[]{:S(2)}, u32[]{:S(2)}) collective-permute-start(bf16[264,128]{1,0:T(8,128)(2,1)S(1)} %collective-permute-done.3.refs_6_), channel_id=1, source_target_pairs={{0,1},{1,0},{2,3},{3,2},{4,5},{5,4},{6,7},{7,6},{8,10},{9,11},{10,... | collective-permute-start | bytes 202760 | tf_op jit(solution)/shard_map/ppermute | solution.py:285
  9.2 0.0 collective-permute-done.1.refs_4_
  9.2 0.5 %collective-permute-start.5 = (bf16[264,128]{1,0:T(8,128)(2,1)S(1)}, bf16[264,128]{1,0:T(8,128)(2,1)S(1)}, u32[]{:S(2)}, u32[]{:S(2)}) collective-permute-start(bf16[264,128]{1,0:T(8,128)(2,1)S(1)} %collective-permute-done.1.refs_4_), channel_id=1, source_target_pairs={{0,1},{1,0},{2,3},{3,2},{4,6},{5,7},{6,4},{7,5},{8,9},{9,8},{10,11... | collective-permute-start | bytes 202760 | tf_op jit(solution)/shard_map/ppermute | solution.py:285
  9.7 0.0 collective-permute-done.2.refs_5_
  9.7 1.5 %collective-permute-start.6 = (bf16[264,128]{1,0:T(8,128)(2,1)S(1)}, bf16[264,128]{1,0:T(8,128)(2,1)S(1)}, u32[]{:S(2)}, u32[]{:S(2)}) collective-permute-start(bf16[264,128]{1,0:T(8,128)(2,1)S(1)} %collective-permute-done.2.refs_5_), channel_id=1, source_target_pairs={{0,1},{1,0},{2,3},{3,2},{4,5},{5,4},{6,7},{7,6},{8,10},{9,11},{10,... | collective-permute-start | bytes 202760 | tf_op jit(solution)/shard_map/ppermute | solution.py:285
  11.2 1.1 %prep.1 = (bf16[1024,128]{1,0:T(8,128)(2,1)S(1)}, f32[128,128]{1,0:T(8,128)S(1)}) custom-call(bf16[128,512]{1,0:T(8,128)(2,1)} %q_hbm.1, bf16[264,128]{1,0:T(8,128)(2,1)S(1)} %pack.1.own.refs_2_), custom_call_target="tpu_custom_call" | custom-call | tf_op jit(solution)/shard_map/prep/pallas_call | solution.py:291
  12.4 0.0 collective-permute-done.refs_3_
  12.4 0.0 collective-permute-done.4.refs_7_
  12.4 1.8 %near.1 = (f32[1024,128]{1,0:T(8,128)S(1)}, f32[1024,128]{1,0:T(8,128)S(1)}, f32[1024,128]{1,0:T(8,128)S(1)}, bf16[128,512]{1,0:T(8,128)(2,1)}) custom-call(bf16[1024,128]{1,0:T(8,128)(2,1)S(1)} %get-tuple-element.11.refs_0_, f32[128,128]{1,0:T(8,128)S(1)} %get-tuple-element.12.refs_1_, bf16[264,128]{1,0:T(8,128)(2,1)S(1)} %pack.1.own.refs_2_, ...), custom_call_target="tpu_custom_call" | custom-call | tf_op jit(solution)/shard_map/near/pallas_call | solution.py:306
  14.1 0.0 collective-permute-done.5.refs_6_
  14.2 0.0 collective-permute-done.6.refs_7_
  14.2 1.6 %far.1 = bf16[128,512]{1,0:T(8,128)(2,1)} custom-call(bf16[1024,128]{1,0:T(8,128)(2,1)S(1)} %get-tuple-element.11.refs_0_, f32[128,128]{1,0:T(8,128)S(1)} %get-tuple-element.12.refs_1_, f32[1024,128]{1,0:T(8,128)S(1)} %get-tuple-element.13.refs_2_, f32[1024,128]{1,0:T(8,128)S(1)} %get-tuple-element.14.refs_3_, ...), custom_call_target="tpu_custom_call", output_to_operand_aliasing={{}: (5, {})} | custom-call | tf_op jit(solution)/shard_map/far/pallas_call | solution.py:324
Async XLA Ops:
  0.8 6.9 %collective-permute-start.3 = (bf16[264,128]{1,0:T(8,128)(2,1)S(1)}, bf16[264,128]{1,0:T(8,128)(2,1)S(1)}, u32[]{:S(2)}, u32[]{:S(2)}) collective-permute-start(bf16[264,128]{1,0:T(8,128)(2,1)S(1)} %pack.1.own.refs_2_), channel_id=1, source_target_pairs={{0,12},{1,13},{2,14},{3,15},{4,8},{5,9},{6,10},{7,11},{8,4},{9,5},... | collective-permute-start | bytes 202760 | tf_op jit(solution)/shard_map/ppermute | solution.py:285
  0.9 8.3 %collective-permute-start.1 = (bf16[264,128]{1,0:T(8,128)(2,1)S(1)}, bf16[264,128]{1,0:T(8,128)(2,1)S(1)}, u32[]{:S(2)}, u32[]{:S(2)}) collective-permute-start(bf16[264,128]{1,0:T(8,128)(2,1)S(1)} %pack.1.own.refs_2_), channel_id=1, source_target_pairs={{0,4},{1,5},{2,6},{3,7},{4,0},{5,1},{6,2},{7,3},{8,12},{9,13},{10,... | collective-permute-start | bytes 202760 | tf_op jit(solution)/shard_map/ppermute | solution.py:285
  1.8 7.9 %collective-permute-start.2 = (bf16[264,128]{1,0:T(8,128)(2,1)S(1)}, bf16[264,128]{1,0:T(8,128)(2,1)S(1)}, u32[]{:S(2)}, u32[]{:S(2)}) collective-permute-start(bf16[264,128]{1,0:T(8,128)(2,1)S(1)} %pack.1.own.refs_2_), channel_id=1, source_target_pairs={{0,8},{1,9},{2,10},{3,11},{4,12},{5,13},{6,14},{7,15},{8,0},{9,1},... | collective-permute-start | bytes 202760 | tf_op jit(solution)/shard_map/ppermute | solution.py:285
  5.3 7.1 %collective-permute-start = (bf16[264,128]{1,0:T(8,128)(2,1)S(1)}, bf16[264,128]{1,0:T(8,128)(2,1)S(1)}, u32[]{:S(2)}, u32[]{:S(2)}) collective-permute-start(bf16[264,128]{1,0:T(8,128)(2,1)S(1)} %pack.1.own.refs_2_), channel_id=1, source_target_pairs={{0,2},{1,3},{2,0},{3,1},{4,6},{5,7},{6,4},{7,5},{8,10},{9,11},{10,... | collective-permute-start | bytes 202760 | tf_op jit(solution)/shard_map/ppermute | solution.py:285
  7.7 4.7 %collective-permute-start.4 = (bf16[264,128]{1,0:T(8,128)(2,1)S(1)}, bf16[264,128]{1,0:T(8,128)(2,1)S(1)}, u32[]{:S(2)}, u32[]{:S(2)}) collective-permute-start(bf16[264,128]{1,0:T(8,128)(2,1)S(1)} %collective-permute-done.3.refs_6_), channel_id=1, source_target_pairs={{0,1},{1,0},{2,3},{3,2},{4,5},{5,4},{6,7},{7,6},{8,10},{9,11},{10,... | collective-permute-start | bytes 202760 | tf_op jit(solution)/shard_map/ppermute | solution.py:285
  9.2 5.0 %collective-permute-start.5 = (bf16[264,128]{1,0:T(8,128)(2,1)S(1)}, bf16[264,128]{1,0:T(8,128)(2,1)S(1)}, u32[]{:S(2)}, u32[]{:S(2)}) collective-permute-start(bf16[264,128]{1,0:T(8,128)(2,1)S(1)} %collective-permute-done.1.refs_4_), channel_id=1, source_target_pairs={{0,1},{1,0},{2,3},{3,2},{4,6},{5,7},{6,4},{7,5},{8,9},{9,8},{10,11... | collective-permute-start | bytes 202760 | tf_op jit(solution)/shard_map/ppermute | solution.py:285
  9.7 4.5 %collective-permute-start.6 = (bf16[264,128]{1,0:T(8,128)(2,1)S(1)}, bf16[264,128]{1,0:T(8,128)(2,1)S(1)}, u32[]{:S(2)}, u32[]{:S(2)}) collective-permute-start(bf16[264,128]{1,0:T(8,128)(2,1)S(1)} %collective-permute-done.2.refs_5_), channel_id=1, source_target_pairs={{0,1},{1,0},{2,3},{3,2},{4,5},{5,4},{6,7},{7,6},{8,10},{9,11},{10,... | collective-permute-start | bytes 202760 | tf_op jit(solution)/shard_map/ppermute | solution.py:285

commit v4 on v3

--- a/solution.py
+++ b/solution.py
@@ -185,80 +185,75 @@
         q_all[head * tokens : (head + 1) * tokens, :] = jnp.where(keep, tile, 0.0).astype(jnp.bfloat16)
 
 
-def near_steps(count):
-    return [0, 1] + list(range(2, count, 2)) + [count - 1]
-
-
-def far_steps(count):
-    return list(range(3, count - 1, 2))
-
-
-def near_kernel(groups, repeat, count, *refs):
-    steps = near_steps(count)
+def stages_of(count):
+    forwarded = [step for step, _, _ in plan_of(count) if step > 1 and step % 2]
+    return [[0, 1] + list(range(2, count, 2)), forwarded[:-1], forwarded[-1:]]
+
+
+def stage_kernel(groups, repeat, count, number, *refs):
+    stages = stages_of(count)
+    steps = stages[number]
     q_all, seg_ref, pieces = refs[0], refs[1], dict(zip(steps, refs[2 : 2 + len(steps)]))
-    top_ref, sum_ref, mix_ref, out_hbm, out_buf, scores, sems = refs[2 + len(steps) :]
+    top_ref, sum_ref, mix_ref, out_hbm, out_buf, scores, sems = refs[-7:]
     lanes = q_all.shape[1]
     tokens = seg_ref.shape[0]
     width = lanes // groups
     heads = groups * repeat
     factor = math.log2(math.e) / math.sqrt(width)
     me = lax.axis_index("seq")
-    query_seg = seg_ref[...]
 
     for pair in range(count // 2):
+        early = seen_steps(pair, count)
+        seen = [[step for step in stage if step < 2 or step & -2 in early] for stage in stages]
+        if not seen[number]:
+            continue
 
         @pl.when(me // 2 == pair)
-        def _(pair=pair):
-            early = seen_steps(pair, count)
-            chosen = [step for step in steps if step < 2 or step & -2 in early]
-            blocks = paired([(step, pieces[step]) for step in chosen])
+        def _(seen=seen):
+            more = any(seen[number + 1 :])
             output = Output(repeat, width, lanes, out_buf, out_hbm, sems)
 
+            def before(rows):
+                if number == 0:
+                    return None
+                return top_ref[rows, :], sum_ref[rows, :], mix_ref[rows, :]
+
             def after(head, rows, top, total, mixed):
-                if early:
+                if more:
                     top_ref[rows, :] = jnp.broadcast_to(top, (tokens, lanes))
                     sum_ref[rows, :] = total
                     mix_ref[rows, :] = mixed
                 else:
                     output.add(normal(total, mixed))
 
-            attend(me, blocks, query_seg, q_all, scores, heads, factor, lambda rows: None, after)
-            output.finish()
-
-
-def far_kernel(groups, repeat, count, *refs):
-    steps = far_steps(count)
-    q_all, seg_ref, top_ref, sum_ref, mix_ref, out_in = refs[:6]
-    pieces = dict(zip(steps, refs[6 : 6 + len(steps)]))
-    out_hbm, out_buf, scores, sems = refs[6 + len(steps) :]
-    del out_in
-    lanes = q_all.shape[1]
-    width = lanes // groups
-    heads = groups * repeat
-    factor = math.log2(math.e) / math.sqrt(width)
-    me = lax.axis_index("seq")
-
-    for pair in range(1, count // 2):
-
-        @pl.when(me // 2 == pair)
-        def _(pair=pair):
-            early = seen_steps(pair, count)
-            blocks = paired([(step, pieces[step]) for step in steps if step & -2 in early])
-            output = Output(repeat, width, lanes, out_buf, out_hbm, sems)
-
-            def before(rows):
-                return top_ref[rows, :], sum_ref[rows, :], mix_ref[rows, :]
-
-            def after(head, rows, top, total, mixed):
-                output.add(normal(total, mixed))
-
+            blocks = paired([(step, pieces[step]) for step in seen[number]])
             attend(me, blocks, seg_ref[...], q_all, scores, heads, factor, before, after)
             output.finish()
 
 
-def partners(count, cores, step, mask):
+def stage_call(groups, repeat, count, number, queries, q_all, query_seg, pieces, carried):
+    rows, lanes = q_all.shape
+    tokens = query_seg.shape[0]
+    state = pltpu.VMEM((rows, lanes), jnp.float32)
+    first = 2 + len(pieces)
+    return pl.pallas_call(
+        functools.partial(stage_kernel, groups, repeat, count, number),
+        out_shape=[state, state, state, pltpu.HBM(queries.shape, queries.dtype)],
+        in_specs=[VMEM] * first + ([VMEM] * 3 + [HBM] if carried else []),
+        out_specs=[VMEM] * 3 + [HBM],
+        scratch_shapes=[
+            pltpu.VMEM((tokens, queries.shape[1]), queries.dtype),
+            pltpu.VMEM(((len(pieces) + 1) // 2, rows, 2 * tokens), jnp.float32),
+            pltpu.SemaphoreType.DMA((queries.shape[1] // lanes,)),
+        ],
+        input_output_aliases={first + at: at for at in range(4)} if carried else {},
+        compiler_params=pltpu.CompilerParams(vmem_limit_bytes=VMEM_LIMIT),
+    )(q_all, query_seg, *pieces, *carried)
+
+
+def partners(count, cores, step, source, mask):
     def needs(i):
-        return step < 2 or step % 2 == 0 or (i ^ step) // 2 < i // 2
+        return source == 0 or (i ^ step) // 2 < i // 2
 
     pairs = []
     for i in range(count):
@@ -282,11 +277,8 @@
     plan = plan_of(count)
     held = {0: pack(key_matrix, value_matrix, segment_ids.reshape(1, tokens))}
     for step, source, mask in plan:
-        held[step] = lax.ppermute(held[source], ("seq", "head"), partners(count, cores, step, mask))
-    near = near_steps(count)
-    far = far_steps(count)
+        held[step] = lax.ppermute(held[source], ("seq", "head"), partners(count, cores, step, source, mask))
     row_shape = (heads * tokens, lanes)
-    score_shape = (heads * tokens, 2 * tokens)
     tiles = queries.shape[1] // lanes
     q_all, query_seg = pl.pallas_call(
         functools.partial(prep_kernel, groups, repeat),
@@ -303,38 +295,13 @@
         compiler_params=pltpu.CompilerParams(vmem_limit_bytes=SMALL_VMEM),
         name="prep",
     )(in_hbm(queries), held[0])
-    top, total, mixed, out = pl.pallas_call(
-        functools.partial(near_kernel, groups, repeat, count),
-        out_shape=[
-            pltpu.VMEM(row_shape, jnp.float32),
-            pltpu.VMEM(row_shape, jnp.float32),
-            pltpu.VMEM(row_shape, jnp.float32),
-            pltpu.HBM(queries.shape, queries.dtype),
-        ],
-        in_specs=[VMEM] * (2 + len(near)),
-        out_specs=[VMEM] * 3 + [HBM],
-        scratch_shapes=[
-            pltpu.VMEM(queries.shape, queries.dtype),
-            pltpu.VMEM(((len(near) + 1) // 2,) + score_shape, jnp.float32),
-            pltpu.SemaphoreType.DMA((tiles,)),
-        ],
-        compiler_params=pltpu.CompilerParams(vmem_limit_bytes=VMEM_LIMIT),
-        name="near",
-    )(q_all, query_seg, *[held[step] for step in near])
-    return pl.pallas_call(
-        functools.partial(far_kernel, groups, repeat, count),
-        out_shape=pltpu.HBM(queries.shape, queries.dtype),
-        in_specs=[VMEM] * 5 + [HBM] + [VMEM] * len(far),
-        out_specs=HBM,
-        scratch_shapes=[
-            pltpu.VMEM(queries.shape, queries.dtype),
-            pltpu.VMEM(((len(far) + 1) // 2,) + score_shape, jnp.float32),
-            pltpu.SemaphoreType.DMA((tiles,)),
-        ],
-        input_output_aliases={5: 0},
-        compiler_params=pltpu.CompilerParams(vmem_limit_bytes=VMEM_LIMIT),
-        name="far",
-    )(q_all, query_seg, top, total, mixed, out, *[held[step] for step in far])
+    carried = []
+    for number, steps in enumerate(stages_of(count)):
+        carried = stage_call(
+            groups, repeat, count, number, queries, q_all, query_seg,
+            [held[step] for step in steps], carried,
+        )
+    return carried[-1]
 
 
 def attend_block(state, query_heads, query_pos, query_seg, key_blk, value_blk, seg_blk, key_start):

time: 16.1 us -> 17.1 us (1.062)
  the two profiles are of different devices: /device:TPU:24 before, /device:TPU:16 now
where the time goes in v4:
time: 17.1 us; the launch traced here: 16.8 us
  starting transfers between devices  7.97 us (47%)
  Pallas kernels  4.94 us (29%)
  waiting for transfers between devices  3.84 us (22%)
    ppermute x7, starting transfers between devices, per_device(): lax.ppermute(held[source], ('seq', 'head'), partners(count, cores, step,...  7.97 us
    ppermute x7, waiting for transfers between devices, per_device(): lax.ppermute(held[source], ('seq', 'head'), partners(count, cores, step,...  3.84 us
    pallas_call x3, Pallas kernels, stage_call(): pl.pallas_call(functools.partial(stage_kernel, groups, repeat, count, num...  3 us
    pallas_call x1, Pallas kernels, per_device(): pl.pallas_call(functools.partial(prep_kernel, groups, repeat), out_shape=...  1.12 us
    pallas_call x1, Pallas kernels, pack(): pl.pallas_call(pack_kernel, out_shape=pltpu.VMEM((2 * tokens + SEG_ROWS,...  0.81 us
  transfers between devices with their start and end apart: 7, of which 2 were waited for; matrix products, arithmetic and copies ran while one was open for 0% of the time, Pallas kernels for 17%

profile of v4, /device:TPU:16, one launch (start us, length us, event | category | flops | bytes accessed | tf_op | source)
XLA Modules:
  0.0 16.8 jit_solution(14731448274535051410)
XLA Ops:
  0.0 0.8 %pack.1.own.refs_2_ = bf16[264,128]{1,0:T(8,128)(2,1)S(1)} custom-call(bf16[128,128]{1,0:T(8,128)(2,1)} %k_ref.1, bf16[128,128]{1,0:T(8,128)(2,1)} %v_ref.1, s32[1,128]{1,0:T(1,128)} %bitcast.1), custom_call_target="tpu_custom_call" | custom-call | tf_op jit(solution)/shard_map/pack/pallas_call | solution.py:43
  0.8 1.6 %collective-permute-start.4 = (bf16[264,128]{1,0:T(8,128)(2,1)S(1)}, bf16[264,128]{1,0:T(8,128)(2,1)S(1)}, u32[]{:S(2)}, u32[]{:S(2)}) collective-permute-start(bf16[264,128]{1,0:T(8,128)(2,1)S(1)} %pack.1.own.refs_2_), channel_id=1, source_target_pairs={{0,4},{1,5},{2,6},{3,7},{4,0},{5,1},{6,2},{7,3},{8,12},{9,13},{10,... | collective-permute-start | bytes 202760 | tf_op jit(solution)/shard_map/ppermute | solution.py:280
  2.5 0.0 collective-permute-start.2
  2.5 2.8 %collective-permute-start = (bf16[264,128]{1,0:T(8,128)(2,1)S(1)}, bf16[264,128]{1,0:T(8,128)(2,1)S(1)}, u32[]{:S(2)}, u32[]{:S(2)}) collective-permute-start(bf16[264,128]{1,0:T(8,128)(2,1)S(1)} %pack.1.own.refs_2_), channel_id=1, source_target_pairs={{0,8},{1,9},{2,10},{3,11},{4,12},{5,13},{6,14},{7,15},{8,0},{9,1},... | collective-permute-start | bytes 202760 | tf_op jit(solution)/shard_map/ppermute | solution.py:280
  5.3 1.5 %collective-permute-start.6 = (bf16[264,128]{1,0:T(8,128)(2,1)S(1)}, bf16[264,128]{1,0:T(8,128)(2,1)S(1)}, u32[]{:S(2)}, u32[]{:S(2)}) collective-permute-start(bf16[264,128]{1,0:T(8,128)(2,1)S(1)} %pack.1.own.refs_2_), channel_id=1, source_target_pairs={{0,2},{1,3},{2,0},{3,1},{4,6},{5,7},{6,4},{7,5},{8,10},{9,11},{10,... | collective-permute-start | bytes 202760 | tf_op jit(solution)/shard_map/ppermute | solution.py:280
  6.8 0.0 collective-permute-done.4.refs_4_
  6.8 0.0 collective-permute-start.5
  6.8 3.0 %collective-permute-done.2.refs_6_ = bf16[264,128]{1,0:T(8,128)(2,1)S(1)} collective-permute-done((bf16[264,128]{1,0:T(8,128)(2,1)S(1)}, bf16[264,128]{1,0:T(8,128)(2,1)S(1)}, u32[]{:S(2)}, u32[]{:S(2)}) %collective-permute-start.2) | collective-permute-done | bytes 67616 | tf_op jit(solution)/shard_map/ppermute | solution.py:280
  9.7 1.5 %collective-permute-start.3 = (bf16[264,128]{1,0:T(8,128)(2,1)S(1)}, bf16[264,128]{1,0:T(8,128)(2,1)S(1)}, u32[]{:S(2)}, u32[]{:S(2)}) collective-permute-start(bf16[264,128]{1,0:T(8,128)(2,1)S(1)} %collective-permute-done.2.refs_6_), channel_id=1, source_target_pairs={{0,1},{1,0},{2,3},{3,2},{4,5},{5,4},{6,7},{7,6},{8,10},{9,11},{10,... | collective-permute-start | bytes 202760 | tf_op jit(solution)/shard_map/ppermute | solution.py:280
  11.2 0.0 collective-permute-done.refs_5_
  11.2 0.5 %collective-permute-start.1 = (bf16[264,128]{1,0:T(8,128)(2,1)S(1)}, bf16[264,128]{1,0:T(8,128)(2,1)S(1)}, u32[]{:S(2)}, u32[]{:S(2)}) collective-permute-start(bf16[264,128]{1,0:T(8,128)(2,1)S(1)} %collective-permute-done.refs_5_), channel_id=1, source_target_pairs={{0,1},{1,0},{2,3},{3,2},{4,5},{5,4},{6,7},{7,6},{8,10},{9,11},{10,... | collective-permute-start | bytes 202760 | tf_op jit(solution)/shard_map/ppermute | solution.py:280
  11.8 1.1 %prep.1 = (bf16[1024,128]{1,0:T(8,128)(2,1)S(1)}, f32[128,128]{1,0:T(8,128)S(1)}) custom-call(bf16[128,512]{1,0:T(8,128)(2,1)} %q_hbm.1, bf16[264,128]{1,0:T(8,128)(2,1)S(1)} %pack.1.own.refs_2_), custom_call_target="tpu_custom_call" | custom-call | tf_op jit(solution)/shard_map/prep/pallas_call | solution.py:283
  12.9 0.0 collective-permute-done.6.refs_3_
  12.9 1.1 %shard_map.46 = (f32[1024,128]{1,0:T(8,128)S(1)}, f32[1024,128]{1,0:T(8,128)S(1)}, f32[1024,128]{1,0:T(8,128)S(1)}, bf16[128,512]{1,0:T(8,128)(2,1)}) custom-call(bf16[1024,128]{1,0:T(8,128)(2,1)S(1)} %get-tuple-element.16.refs_0_, f32[128,128]{1,0:T(8,128)S(1)} %get-tuple-element.17.refs_1_, bf16[264,128]{1,0:T(8,128)(2,1)S(1)} %pack.1.own.refs_2_, ...), custom_call_target="tpu_custom_call" | custom-call | tf_op jit(solution)/shard_map/pallas_call | solution.py:239
  14.0 0.0 collective-permute-done.5.refs_3_
  14.1 0.0 collective-permute-done.3.refs_2_
  14.1 0.6 %shard_map.47 = (f32[1024,128]{1,0:T(8,128)S(1)}, f32[1024,128]{1,0:T(8,128)S(1)}, f32[1024,128]{1,0:T(8,128)S(1)}, bf16[128,512]{1,0:T(8,128)(2,1)}) custom-call(bf16[1024,128]{1,0:T(8,128)(2,1)S(1)} %get-tuple-element.16.refs_0_, ...), custom_call_target="tpu_custom_call", output_to_operand_aliasing={{0}: (4, {}), {1}: (5, {}), {2}: (6, {}), {3}: (7, {})} | custom-call | tf_op jit(solution)/shard_map/pallas_call | solution.py:239
  14.7 0.9 %collective-permute-done.1.refs_2_ = bf16[264,128]{1,0:T(8,128)(2,1)S(1)} collective-permute-done((bf16[264,128]{1,0:T(8,128)(2,1)S(1)}, bf16[264,128]{1,0:T(8,128)(2,1)S(1)}, u32[]{:S(2)}, u32[]{:S(2)}) %collective-permute-start.1) | collective-permute-done | bytes 67616 | tf_op jit(solution)/shard_map/ppermute | solution.py:280
  15.5 1.3 %shard_map.48 = (f32[1024,128]{1,0:T(8,128)S(1)}, f32[1024,128]{1,0:T(8,128)S(1)}, f32[1024,128]{1,0:T(8,128)S(1)}, bf16[128,512]{1,0:T(8,128)(2,1)}) custom-call(bf16[1024,128]{1,0:T(8,128)(2,1)S(1)} %get-tuple-element.16.refs_0_, ...), custom_call_target="tpu_custom_call", output_to_operand_aliasing={{0}: (3, {}), {1}: (4, {}), {2}: (5, {}), {3}: (6, {})} | custom-call | tf_op jit(solution)/shard_map/pallas_call | solution.py:239
Async XLA Ops:
  0.8 5.9 %collective-permute-start.4 = (bf16[264,128]{1,0:T(8,128)(2,1)S(1)}, bf16[264,128]{1,0:T(8,128)(2,1)S(1)}, u32[]{:S(2)}, u32[]{:S(2)}) collective-permute-start(bf16[264,128]{1,0:T(8,128)(2,1)S(1)} %pack.1.own.refs_2_), channel_id=1, source_target_pairs={{0,4},{1,5},{2,6},{3,7},{4,0},{5,1},{6,2},{7,3},{8,12},{9,13},{10,... | collective-permute-start | bytes 202760 | tf_op jit(solution)/shard_map/ppermute | solution.py:280
  2.5 7.3 %collective-permute-start.2 = (bf16[264,128]{1,0:T(8,128)(2,1)S(1)}, bf16[264,128]{1,0:T(8,128)(2,1)S(1)}, u32[]{:S(2)}, u32[]{:S(2)}) collective-permute-start(bf16[264,128]{1,0:T(8,128)(2,1)S(1)} %pack.1.own.refs_2_), channel_id=1, source_target_pairs={{0,12},{1,13},{2,14},{3,15},{4,8},{5,9},{6,10},{7,11},{8,4},{9,5},... | collective-permute-start | bytes 202760 | tf_op jit(solution)/shard_map/ppermute | solution.py:280
  2.5 8.8 %collective-permute-start = (bf16[264,128]{1,0:T(8,128)(2,1)S(1)}, bf16[264,128]{1,0:T(8,128)(2,1)S(1)}, u32[]{:S(2)}, u32[]{:S(2)}) collective-permute-start(bf16[264,128]{1,0:T(8,128)(2,1)S(1)} %pack.1.own.refs_2_), channel_id=1, source_target_pairs={{0,8},{1,9},{2,10},{3,11},{4,12},{5,13},{6,14},{7,15},{8,0},{9,1},... | collective-permute-start | bytes 202760 | tf_op jit(solution)/shard_map/ppermute | solution.py:280
  5.3 7.6 %collective-permute-start.6 = (bf16[264,128]{1,0:T(8,128)(2,1)S(1)}, bf16[264,128]{1,0:T(8,128)(2,1)S(1)}, u32[]{:S(2)}, u32[]{:S(2)}) collective-permute-start(bf16[264,128]{1,0:T(8,128)(2,1)S(1)} %pack.1.own.refs_2_), channel_id=1, source_target_pairs={{0,2},{1,3},{2,0},{3,1},{4,6},{5,7},{6,4},{7,5},{8,10},{9,11},{10,... | collective-permute-start | bytes 202760 | tf_op jit(solution)/shard_map/ppermute | solution.py:280
  6.8 7.3 %collective-permute-start.5 = (bf16[264,128]{1,0:T(8,128)(2,1)S(1)}, bf16[264,128]{1,0:T(8,128)(2,1)S(1)}, u32[]{:S(2)}, u32[]{:S(2)}) collective-permute-start(bf16[264,128]{1,0:T(8,128)(2,1)S(1)} %collective-permute-done.4.refs_4_), channel_id=1, source_target_pairs={{0,1},{1,0},{2,3},{3,2},{4,6},{5,7},{6,4},{7,5},{8,9},{9,8},{10,11... | collective-permute-start | bytes 202760 | tf_op jit(solution)/shard_map/ppermute | solution.py:280
  9.7 4.3 %collective-permute-start.3 = (bf16[264,128]{1,0:T(8,128)(2,1)S(1)}, bf16[264,128]{1,0:T(8,128)(2,1)S(1)}, u32[]{:S(2)}, u32[]{:S(2)}) collective-permute-start(bf16[264,128]{1,0:T(8,128)(2,1)S(1)} %collective-permute-done.2.refs_6_), channel_id=1, source_target_pairs={{0,1},{1,0},{2,3},{3,2},{4,5},{5,4},{6,7},{7,6},{8,10},{9,11},{10,... | collective-permute-start | bytes 202760 | tf_op jit(solution)/shard_map/ppermute | solution.py:280
  11.2 4.3 %collective-permute-start.1 = (bf16[264,128]{1,0:T(8,128)(2,1)S(1)}, bf16[264,128]{1,0:T(8,128)(2,1)S(1)}, u32[]{:S(2)}, u32[]{:S(2)}) collective-permute-start(bf16[264,128]{1,0:T(8,128)(2,1)S(1)} %collective-permute-done.refs_5_), channel_id=1, source_target_pairs={{0,1},{1,0},{2,3},{3,2},{4,5},{5,4},{6,7},{7,6},{8,10},{9,11},{10,... | collective-permute-start | bytes 202760 | tf_op jit(solution)/shard_map/ppermute | solution.py:280

commit v5 on v4

--- a/solution.py
+++ b/solution.py
@@ -209,8 +209,12 @@
             continue
 
         @pl.when(me // 2 == pair)
-        def _(seen=seen):
-            more = any(seen[number + 1 :])
+        def _(seen=seen, pair=pair):
+            final = max(at for at in range(len(stages)) if seen[at])
+            tested = final > 0 and all(step >> 1 != pair for step in seen[final])
+            writes = number == final
+            if tested:
+                writes = number >= max(at for at in range(final) if seen[at])
             output = Output(repeat, width, lanes, out_buf, out_hbm, sems)
 
             def before(rows):
@@ -219,16 +223,23 @@
                 return top_ref[rows, :], sum_ref[rows, :], mix_ref[rows, :]
 
             def after(head, rows, top, total, mixed):
-                if more:
+                if number < final:
                     top_ref[rows, :] = jnp.broadcast_to(top, (tokens, lanes))
                     sum_ref[rows, :] = total
                     mix_ref[rows, :] = mixed
-                else:
+                if writes:
                     output.add(normal(total, mixed))
 
-            blocks = paired([(step, pieces[step]) for step in seen[number]])
-            attend(me, blocks, seg_ref[...], q_all, scores, heads, factor, before, after)
-            output.finish()
+            def run():
+                blocks = paired([(step, pieces[step]) for step in seen[number]])
+                attend(me, blocks, seg_ref[...], q_all, scores, heads, factor, before, after)
+                output.finish()
+
+            if number < final or not tested:
+                run()
+            else:
+                parts = [bias_of(me, step, pieces[step], seg_ref[...]) for step in seen[number]]
+                pl.when(jnp.max(functools.reduce(jnp.maximum, parts)) == 0.0)(run)
 
 
 def stage_call(groups, repeat, count, number, queries, q_all, query_seg, pieces, carried):
@@ -266,7 +277,8 @@
 
 def plan_of(count):
     column = [count - 2] + list(range(2, count - 2, 2))
-    return [(step, 0, step) for step in column] + [(1, 0, 1)] + [(step + 1, step, 1) for step in column]
+    onward = column[1:2] + column[:1] + column[2:]
+    return [(step, 0, step) for step in column] + [(1, 0, 1)] + [(step + 1, step, 1) for step in onward]
 
 
 def per_device(count, cores, queries, key_matrix, value_matrix, segment_ids):

time: 17.1 us -> 16.1 us (0.942)
  the two profiles are of different devices: /device:TPU:16 before, /device:TPU:24 now
where the time goes in v5:
time: 16.1 us; the launch traced here: 15.8 us
  starting transfers between devices  9.45 us (59%)
  Pallas kernels  5.35 us (33%)
  waiting for transfers between devices  0.94 us (6%)
    ppermute x7, starting transfers between devices, per_device(): lax.ppermute(held[source], ('seq', 'head'), partners(count, cores, step,...  9.45 us
    pallas_call x3, Pallas kernels, stage_call(): pl.pallas_call(functools.partial(stage_kernel, groups, repeat, count, num...  3.41 us
    pallas_call x1, Pallas kernels, per_device(): pl.pallas_call(functools.partial(prep_kernel, groups, repeat), out_shape=...  1.12 us
    ppermute x7, waiting for transfers between devices, per_device(): lax.ppermute(held[source], ('seq', 'head'), partners(count, cores, step,...  0.94 us
    pallas_call x1, Pallas kernels, pack(): pl.pallas_call(pack_kernel, out_shape=pltpu.VMEM((2 * tokens + SEG_ROWS,...  0.81 us
  transfers between devices with their start and end apart: 7, of which 1 were waited for; matrix products, arithmetic and copies ran while one was open for 0% of the time, Pallas kernels for 27%

profile of v5, /device:TPU:24, one launch (start us, length us, event | category | flops | bytes accessed | tf_op | source)
XLA Modules:
  0.0 15.8 jit_solution(3345447513643475745)
XLA Ops:
  0.0 0.8 %pack.1.own.refs_2_ = bf16[264,128]{1,0:T(8,128)(2,1)S(1)} custom-call(bf16[128,128]{1,0:T(8,128)(2,1)} %k_ref.1, bf16[128,128]{1,0:T(8,128)(2,1)} %v_ref.1, s32[1,128]{1,0:T(1,128)} %bitcast.1), custom_call_target="tpu_custom_call" | custom-call | tf_op jit(solution)/shard_map/pack/pallas_call | solution.py:43
  0.8 0.1 collective-permute-start.4
  0.9 0.9 %collective-permute-start.2 = (bf16[264,128]{1,0:T(8,128)(2,1)S(1)}, bf16[264,128]{1,0:T(8,128)(2,1)S(1)}, u32[]{:S(2)}, u32[]{:S(2)}) collective-permute-start(bf16[264,128]{1,0:T(8,128)(2,1)S(1)} %pack.1.own.refs_2_), channel_id=1, source_target_pairs={{0,4},{1,5},{2,6},{3,7},{4,0},{5,1},{6,2},{7,3},{8,12},{9,13},{10,... | collective-permute-start | bytes 202760 | tf_op jit(solution)/shard_map/ppermute | solution.py:292
  1.8 3.5 %collective-permute-start = (bf16[264,128]{1,0:T(8,128)(2,1)S(1)}, bf16[264,128]{1,0:T(8,128)(2,1)S(1)}, u32[]{:S(2)}, u32[]{:S(2)}) collective-permute-start(bf16[264,128]{1,0:T(8,128)(2,1)S(1)} %pack.1.own.refs_2_), channel_id=1, source_target_pairs={{0,8},{1,9},{2,10},{3,11},{4,12},{5,13},{6,14},{7,15},{8,0},{9,1},... | collective-permute-start | bytes 202760 | tf_op jit(solution)/shard_map/ppermute | solution.py:292
  5.3 1.5 %collective-permute-start.6 = (bf16[264,128]{1,0:T(8,128)(2,1)S(1)}, bf16[264,128]{1,0:T(8,128)(2,1)S(1)}, u32[]{:S(2)}, u32[]{:S(2)}) collective-permute-start(bf16[264,128]{1,0:T(8,128)(2,1)S(1)} %pack.1.own.refs_2_), channel_id=1, source_target_pairs={{0,2},{1,3},{2,0},{3,1},{4,6},{5,7},{6,4},{7,5},{8,10},{9,11},{10,... | collective-permute-start | bytes 202760 | tf_op jit(solution)/shard_map/ppermute | solution.py:292
  6.8 0.9 %collective-permute-done.4.refs_6_ = bf16[264,128]{1,0:T(8,128)(2,1)S(1)} collective-permute-done((bf16[264,128]{1,0:T(8,128)(2,1)S(1)}, bf16[264,128]{1,0:T(8,128)(2,1)S(1)}, u32[]{:S(2)}, u32[]{:S(2)}) %collective-permute-start.4) | collective-permute-done | bytes 67616 | tf_op jit(solution)/shard_map/ppermute | solution.py:292
  7.7 1.5 %collective-permute-start.5 = (bf16[264,128]{1,0:T(8,128)(2,1)S(1)}, bf16[264,128]{1,0:T(8,128)(2,1)S(1)}, u32[]{:S(2)}, u32[]{:S(2)}) collective-permute-start(bf16[264,128]{1,0:T(8,128)(2,1)S(1)} %collective-permute-done.4.refs_6_), channel_id=1, source_target_pairs={{0,1},{1,0},{2,3},{3,2},{4,5},{5,4},{6,7},{7,6},{8,10},{9,11},{10,... | collective-permute-start | bytes 202760 | tf_op jit(solution)/shard_map/ppermute | solution.py:292
  9.2 0.0 collective-permute-done.2.refs_4_
  9.2 0.5 %collective-permute-start.3 = (bf16[264,128]{1,0:T(8,128)(2,1)S(1)}, bf16[264,128]{1,0:T(8,128)(2,1)S(1)}, u32[]{:S(2)}, u32[]{:S(2)}) collective-permute-start(bf16[264,128]{1,0:T(8,128)(2,1)S(1)} %collective-permute-done.2.refs_4_), channel_id=1, source_target_pairs={{0,1},{1,0},{2,3},{3,2},{4,6},{5,7},{6,4},{7,5},{8,9},{9,8},{10,11... | collective-permute-start | bytes 202760 | tf_op jit(solution)/shard_map/ppermute | solution.py:292
  9.7 0.0 collective-permute-done.refs_5_
  9.7 1.5 %collective-permute-start.1 = (bf16[264,128]{1,0:T(8,128)(2,1)S(1)}, bf16[264,128]{1,0:T(8,128)(2,1)S(1)}, u32[]{:S(2)}, u32[]{:S(2)}) collective-permute-start(bf16[264,128]{1,0:T(8,128)(2,1)S(1)} %collective-permute-done.refs_5_), channel_id=1, source_target_pairs={{0,1},{1,0},{2,3},{3,2},{4,5},{5,4},{6,7},{7,6},{8,10},{9,11},{10,... | collective-permute-start | bytes 202760 | tf_op jit(solution)/shard_map/ppermute | solution.py:292
  11.2 1.1 %prep.1 = (bf16[1024,128]{1,0:T(8,128)(2,1)S(1)}, f32[128,128]{1,0:T(8,128)S(1)}) custom-call(bf16[128,512]{1,0:T(8,128)(2,1)} %q_hbm.1, bf16[264,128]{1,0:T(8,128)(2,1)S(1)} %pack.1.own.refs_2_), custom_call_target="tpu_custom_call" | custom-call | tf_op jit(solution)/shard_map/prep/pallas_call | solution.py:295
  12.4 0.0 collective-permute-done.6.refs_3_
  12.4 1.6 %shard_map.46 = (f32[1024,128]{1,0:T(8,128)S(1)}, f32[1024,128]{1,0:T(8,128)S(1)}, f32[1024,128]{1,0:T(8,128)S(1)}, bf16[128,512]{1,0:T(8,128)(2,1)}) custom-call(bf16[1024,128]{1,0:T(8,128)(2,1)S(1)} %get-tuple-element.16.refs_0_, f32[128,128]{1,0:T(8,128)S(1)} %get-tuple-element.17.refs_1_, bf16[264,128]{1,0:T(8,128)(2,1)S(1)} %pack.1.own.refs_2_, ...), custom_call_target="tpu_custom_call" | custom-call | tf_op jit(solution)/shard_map/pallas_call | solution.py:250
  13.9 0.0 collective-permute-done.5.refs_3_
  13.9 0.0 collective-permute-done.3.refs_2_
  14.0 1.6 %shard_map.47 = (f32[1024,128]{1,0:T(8,128)S(1)}, f32[1024,128]{1,0:T(8,128)S(1)}, f32[1024,128]{1,0:T(8,128)S(1)}, bf16[128,512]{1,0:T(8,128)(2,1)}) custom-call(bf16[1024,128]{1,0:T(8,128)(2,1)S(1)} %get-tuple-element.16.refs_0_, ...), custom_call_target="tpu_custom_call", output_to_operand_aliasing={{0}: (4, {}), {1}: (5, {}), {2}: (6, {}), {3}: (7, {})} | custom-call | tf_op jit(solution)/shard_map/pallas_call | solution.py:250
  15.6 0.0 collective-permute-done.1.refs_2_
  15.6 0.2 %shard_map.48 = (f32[1024,128]{1,0:T(8,128)S(1)}, f32[1024,128]{1,0:T(8,128)S(1)}, f32[1024,128]{1,0:T(8,128)S(1)}, bf16[128,512]{1,0:T(8,128)(2,1)}) custom-call(bf16[1024,128]{1,0:T(8,128)(2,1)S(1)} %get-tuple-element.16.refs_0_, ...), custom_call_target="tpu_custom_call", output_to_operand_aliasing={{0}: (3, {}), {1}: (4, {}), {2}: (5, {}), {3}: (6, {})} | custom-call | tf_op jit(solution)/shard_map/pallas_call | solution.py:250
Async XLA Ops:
  0.8 6.9 %collective-permute-start.4 = (bf16[264,128]{1,0:T(8,128)(2,1)S(1)}, bf16[264,128]{1,0:T(8,128)(2,1)S(1)}, u32[]{:S(2)}, u32[]{:S(2)}) collective-permute-start(bf16[264,128]{1,0:T(8,128)(2,1)S(1)} %pack.1.own.refs_2_), channel_id=1, source_target_pairs={{0,12},{1,13},{2,14},{3,15},{4,8},{5,9},{6,10},{7,11},{8,4},{9,5},... | collective-permute-start | bytes 202760 | tf_op jit(solution)/shard_map/ppermute | solution.py:292
  0.9 8.3 %collective-permute-start.2 = (bf16[264,128]{1,0:T(8,128)(2,1)S(1)}, bf16[264,128]{1,0:T(8,128)(2,1)S(1)}, u32[]{:S(2)}, u32[]{:S(2)}) collective-permute-start(bf16[264,128]{1,0:T(8,128)(2,1)S(1)} %pack.1.own.refs_2_), channel_id=1, source_target_pairs={{0,4},{1,5},{2,6},{3,7},{4,0},{5,1},{6,2},{7,3},{8,12},{9,13},{10,... | collective-permute-start | bytes 202760 | tf_op jit(solution)/shard_map/ppermute | solution.py:292
  1.8 7.9 %collective-permute-start = (bf16[264,128]{1,0:T(8,128)(2,1)S(1)}, bf16[264,128]{1,0:T(8,128)(2,1)S(1)}, u32[]{:S(2)}, u32[]{:S(2)}) collective-permute-start(bf16[264,128]{1,0:T(8,128)(2,1)S(1)} %pack.1.own.refs_2_), channel_id=1, source_target_pairs={{0,8},{1,9},{2,10},{3,11},{4,12},{5,13},{6,14},{7,15},{8,0},{9,1},... | collective-permute-start | bytes 202760 | tf_op jit(solution)/shard_map/ppermute | solution.py:292
  5.3 7.1 %collective-permute-start.6 = (bf16[264,128]{1,0:T(8,128)(2,1)S(1)}, bf16[264,128]{1,0:T(8,128)(2,1)S(1)}, u32[]{:S(2)}, u32[]{:S(2)}) collective-permute-start(bf16[264,128]{1,0:T(8,128)(2,1)S(1)} %pack.1.own.refs_2_), channel_id=1, source_target_pairs={{0,2},{1,3},{2,0},{3,1},{4,6},{5,7},{6,4},{7,5},{8,10},{9,11},{10,... | collective-permute-start | bytes 202760 | tf_op jit(solution)/shard_map/ppermute | solution.py:292
  7.7 6.2 %collective-permute-start.5 = (bf16[264,128]{1,0:T(8,128)(2,1)S(1)}, bf16[264,128]{1,0:T(8,128)(2,1)S(1)}, u32[]{:S(2)}, u32[]{:S(2)}) collective-permute-start(bf16[264,128]{1,0:T(8,128)(2,1)S(1)} %collective-permute-done.4.refs_6_), channel_id=1, source_target_pairs={{0,1},{1,0},{2,3},{3,2},{4,5},{5,4},{6,7},{7,6},{8,10},{9,11},{10,... | collective-permute-start | bytes 202760 | tf_op jit(solution)/shard_map/ppermute | solution.py:292
  9.2 4.8 %collective-permute-start.3 = (bf16[264,128]{1,0:T(8,128)(2,1)S(1)}, bf16[264,128]{1,0:T(8,128)(2,1)S(1)}, u32[]{:S(2)}, u32[]{:S(2)}) collective-permute-start(bf16[264,128]{1,0:T(8,128)(2,1)S(1)} %collective-permute-done.2.refs_4_), channel_id=1, source_target_pairs={{0,1},{1,0},{2,3},{3,2},{4,6},{5,7},{6,4},{7,5},{8,9},{9,8},{10,11... | collective-permute-start | bytes 202760 | tf_op jit(solution)/shard_map/ppermute | solution.py:292
  9.7 5.9 %collective-permute-start.1 = (bf16[264,128]{1,0:T(8,128)(2,1)S(1)}, bf16[264,128]{1,0:T(8,128)(2,1)S(1)}, u32[]{:S(2)}, u32[]{:S(2)}) collective-permute-start(bf16[264,128]{1,0:T(8,128)(2,1)S(1)} %collective-permute-done.refs_5_), channel_id=1, source_target_pairs={{0,1},{1,0},{2,3},{3,2},{4,5},{5,4},{6,7},{7,6},{8,10},{9,11},{10,... | collective-permute-start | bytes 202760 | tf_op jit(solution)/shard_map/ppermute | solution.py:292
